TPU v7x, 256 devices: a whole 4x4x8 slice. The times are simulated.
256 devices in a mesh: section: 4 (over y), owner: 64 (over x, z, core).
Axes of the slice: x: 4, y: 4, z: 8, core: 2. Of those that a mesh axis runs over, the one named last changes fastest.
Arguments:
- weights: bfloat16 [4, 1024, 1024], P('section'), may hold values from -0.1875 to 0.1875
- inputs: bfloat16 [4, 4, 16384, 1024], P('section', None, 'owner'), may hold values from -16 to 16
- preact: bfloat16 [4, 4, 16384, 1024], P('section', None, 'owner'), may hold values from -6 to 6
- cotangent: bfloat16 [4, 16384, 1024], P(None, 'owner'), may hold values from -6 to 6
- embeddings: bfloat16 [4, 16384, 32, 128], P(None, ('owner', 'section')), may hold values from -6 to 6
- row_ids: int32 [4, 16384, 32], P(None, ('owner', 'section')), may hold values from 0 to 1023
Outputs:
- weight_grad: float32 [4, 1024, 1024], P('section', 'owner')
- table_grad: float32 [64, 512, 128], P('owner', 'section')
All inputs are finite; a program needn't handle non-finite values.
Results may differ from a plain program's by a relative error of at most 0.0064.
Values may be sent and summed in bfloat16 or wider, within the bound.
A program may use at most 128 MiB of HBM per device.

v0:
```python
import math

import jax
import jax.numpy as jnp
from jax import lax
from jax.sharding import Mesh
from jax.sharding import PartitionSpec as P

TROWS = 512
OWNER = ("owner_0", "owner_1", "owner_2")
OWNER_SECTION = ("owner_0", "owner_1", "owner_2", "section")


def partner(block, axis, apart):
    count = lax.axis_size(axis)
    route = []
    for low in range(count):
        high = low | 1 << apart
        if high != low and high < count:
            route += [(low, high), (high, low)]
    return lax.ppermute(block, axis, route)


def passed_along(x, axis, by):
    count = lax.axis_size(axis)
    pairs = [(i, i + by) for i in range(count) if 0 <= i + by < count]
    return lax.ppermute(x, axis, pairs)


def cut_along(x, dim, count):
    lengths = x.shape
    parts = x.reshape(*lengths[:dim], count, lengths[dim] // count, *lengths[dim + 1 :])
    return jnp.moveaxis(parts, dim, 0)


def sum_at_owner(x, axis, dim):
    count = lax.axis_size(axis)
    parts = lax.all_to_all(cut_along(x, dim, count), axis, 0, 0, tiled=True)
    return jnp.sum(parts.astype(jnp.float32), axis=0)


def summed_on_arrival(x, axis, dim):
    count = lax.axis_size(axis)
    parts = lax.all_to_all(cut_along(x, dim, count), axis, 0, 0, tiled=True)
    return jnp.sum(parts, axis=0)


def sum_in_order(parts, axes, sequence):
    lengths = [lax.axis_size(a) for a in axes]
    parts = parts.reshape(*lengths, *parts.shape[1:])
    parts = parts.transpose(*sequence, *range(len(axes), parts.ndim))
    parts = parts.reshape(-1, *parts.shape[len(axes) :])
    for k in sequence:
        parts = lax.psum_scatter(parts, axes[k], scatter_dimension=0, tiled=True)
    return parts[0]


def sum_by_axis(x, axes, sequence, dim):
    count = lax.axis_size(axes)
    return sum_in_order(cut_along(x, dim, count), axes, sequence)


def pair_grads(flat_grad, embedded, features):
    sample_count = flat_grad.shape[0]
    square = flat_grad.reshape(sample_count, features, features)
    direct = jnp.einsum("qfg,qge->qfe", square, embedded, preferred_element_type=jnp.float32)
    swapped = jnp.einsum("qgf,qge->qfe", square, embedded, preferred_element_type=jnp.float32)
    return (direct + swapped).astype(jnp.bfloat16)


def spread_slots(feat_grads, feat_ids, row_split):
    sample_count, features, emb_width = feat_grads.shape
    portion_rows = sample_count // row_split
    grads_split = feat_grads.reshape(row_split, portion_rows, features, emb_width)
    grads_split = jnp.transpose(grads_split, (1, 2, 0, 3)).reshape(
        portion_rows, features * row_split, emb_width
    )
    ids_split = feat_ids.reshape(row_split, portion_rows, features)
    ids_split = jnp.transpose(ids_split, (1, 2, 0)).reshape(portion_rows, features * row_split)
    return (grads_split, ids_split)


def scatter_rows(arrived, local_row, row_total):
    sample_count, slot_count, emb_width = arrived.shape
    block_rows = math.gcd(sample_count, 2048)
    turns = sample_count // block_rows
    pieces_all = arrived.reshape(turns, block_rows, slot_count, emb_width)
    places_all = local_row.reshape(turns, block_rows, slot_count)
    positions = jnp.arange(row_total, dtype=jnp.int32)

    def add_block(running, members):
        pieces, places = members
        onehot = (places[..., None] == positions).astype(jnp.bfloat16)
        return (
            running
            + jnp.einsum("qsr,qse->sre", onehot, pieces, preferred_element_type=jnp.float32),
            None,
        )

    start_table = jnp.zeros((slot_count, row_total, emb_width), jnp.float32)
    running, unused = lax.scan(add_block, start_table, (pieces_all, places_all))
    return running


def table_rows(arrived, arrived_ids, row_split):
    return scatter_rows(arrived, arrived_ids, TROWS * row_split)


def settle_rows(partial_value, owner_pos):
    half_rows = partial_value.shape[1] // 2
    lower = partial_value[:, :half_rows]
    upper = partial_value[:, half_rows:]
    upper_side = owner_pos // 2**0 % 2 == 1
    kept = jnp.where(upper_side, upper, lower)
    sending = jnp.where(upper_side, lower, upper)
    partial_value = kept + partner(sending, OWNER, 0)
    return partial_value


def per_device(weights, inputs, preact, cotangent, embeddings, row_ids):
    sections = lax.axis_size("section")
    owners = lax.axis_size(OWNER)
    section_pos = lax.axis_index("section")
    owner_pos = lax.axis_index(OWNER)
    micro_count, batch_rows, hidden = cotangent.shape
    features = embeddings.shape[2]
    emb_width = embeddings.shape[3]
    row_split = max(1, owners // features)
    grad_scale = 1.0 / math.sqrt(micro_count * batch_rows * owners)
    layer_w = weights[0]
    layer_in = inputs[0]
    layer_pre = preact[0]
    is_last = section_pos == sections - 1
    received = jnp.zeros((batch_rows, hidden), jnp.bfloat16)
    slopes = jnp.zeros((micro_count, batch_rows, hidden), jnp.bfloat16)
    section_zero = []
    row_table = 0.0
    moments = micro_count + sections - 1
    for moment in range(moments):
        micro_pos = moment - (sections - 1 - section_pos)
        active = (micro_pos >= 0) & (micro_pos < micro_count)
        clipped = jnp.clip(micro_pos, 0, micro_count - 1)
        fresh = lax.dynamic_index_in_dim(cotangent, clipped, 0, False)
        incoming = jnp.where(is_last, fresh, received)
        pre_now = lax.dynamic_index_in_dim(layer_pre, clipped, 0, False)
        slope = jnp.where(active & (pre_now > 0), incoming, jnp.zeros_like(incoming))
        slopes = jnp.where(
            active, lax.dynamic_update_index_in_dim(slopes, slope, clipped, 0), slopes
        )
        passed = lax.dot_general(
            slope, layer_w, (((1,), (1,)), ((), ())), preferred_element_type=jnp.float32
        ).astype(jnp.bfloat16)
        if moment >= sections - 1:
            from_zero = jnp.where(
                section_pos == 0,
                passed.astype(jnp.float32),
                jnp.zeros((batch_rows, hidden), jnp.float32),
            )
            section_zero.append(from_zero)
        if moment + 1 < moments:
            received = passed_along(passed, "section", -1)
    stacked = jnp.stack(section_zero)
    portion = sum_at_owner(stacked.astype(jnp.bfloat16), "section", 1).astype(jnp.bfloat16)
    quarter = portion.shape[1]
    feat_grads = pair_grads(
        portion.reshape(micro_count * quarter, hidden),
        embeddings.reshape(micro_count * quarter, features, emb_width),
        features,
    )
    outgoing, out_ids = spread_slots(
        feat_grads, row_ids.reshape(micro_count * quarter, features), row_split
    )
    arrived = lax.all_to_all(outgoing, OWNER, split_axis=1, concat_axis=0, tiled=True)
    arrived_ids = lax.all_to_all(out_ids, OWNER, split_axis=1, concat_axis=0, tiled=True)
    row_table = table_rows(arrived, arrived_ids, row_split)
    row_table = settle_rows(row_table, owner_pos)
    table_grad = summed_on_arrival(row_table, "section", 1) * grad_scale
    flat_in = layer_in.reshape(micro_count * batch_rows, hidden)
    flat_slope = slopes.reshape(micro_count * batch_rows, hidden)
    weight_grad = (
        sum_by_axis(
            lax.dot_general(
                flat_in, flat_slope, (((0,), (0,)), ((), ())), preferred_element_type=jnp.float32
            ),
            OWNER,
            (2, 0, 1),
            0,
        )
        * grad_scale
    )
    return (weight_grad[None], table_grad)


def solution(mesh):
    finer = Mesh(
        mesh.devices.reshape(mesh.shape["section"], 4, 8, 2),
        ("section", "owner_0", "owner_1", "owner_2"),
    )
    placed = (
        P("section", None, None),
        P("section", None, OWNER, None),
        P("section", None, OWNER, None),
        P(None, OWNER, None),
        P(None, OWNER_SECTION, None, None),
        P(None, OWNER_SECTION, None),
    )
    return jax.shard_map(
        per_device,
        mesh=finer,
        in_specs=placed,
        out_specs=(P("section", OWNER, None), P(OWNER, "section", None)),
        check_vma=False,
    )
```

profile of v0, /device:TPU:1, one launch (start us, length us, event | category | flops | bytes accessed | tf_op | source)
XLA Modules:
  0.0 291.8 jit_solution(14479372585268519832)
XLA Ops:
  7.2 2.8 fusion.29
  16.1 7.5 %collective-permute-done = bf16[256,1024]{1,0:T(8,128)(2,1)S(1)} collective-permute-done((bf16[256,1024]{1,0:T(8,128)(2,1)S(1)}, bf16[256,1024]{1,0:T(8,128)(2,1)S(1)}, u32[]{:S(2)}, u32[]{:S(2)}) %collective-permute-start) | collective-permute-done | bytes 524320 | tf_op jit(solution)/shard_map/ppermute | solution.py:27
  28.1 14.4 %collective-permute-done.1 = bf16[256,1024]{1,0:T(8,128)(2,1)S(1)} collective-permute-done((bf16[256,1024]{1,0:T(8,128)(2,1)S(1)}, bf16[256,1024]{1,0:T(8,128)(2,1)S(1)}, u32[]{:S(2)}, u32[]{:S(2)}) %collective-permute-start.1) | collective-permute-done | bytes 524320 | tf_op jit(solution)/shard_map/ppermute | solution.py:27
  42.5 2.6 fusion.65
  47.2 11.7 %collective-permute-done.2 = bf16[256,1024]{1,0:T(8,128)(2,1)S(1)} collective-permute-done((bf16[256,1024]{1,0:T(8,128)(2,1)S(1)}, bf16[256,1024]{1,0:T(8,128)(2,1)S(1)}, u32[]{:S(2)}, u32[]{:S(2)}) %collective-permute-start.2) | collective-permute-done | bytes 524320 | tf_op jit(solution)/shard_map/ppermute | solution.py:27
  58.9 2.6 fusion.64
  64.4 10.8 %collective-permute-done.3 = bf16[256,1024]{1,0:T(8,128)(2,1)S(1)} collective-permute-done((bf16[256,1024]{1,0:T(8,128)(2,1)S(1)}, bf16[256,1024]{1,0:T(8,128)(2,1)S(1)}, u32[]{:S(2)}, u32[]{:S(2)}) %collective-permute-start.3) | collective-permute-done | bytes 524320 | tf_op jit(solution)/shard_map/ppermute | solution.py:27
  80.7 10.0 %collective-permute-done.4 = bf16[256,1024]{1,0:T(8,128)(2,1)S(1)} collective-permute-done((bf16[256,1024]{1,0:T(8,128)(2,1)S(1)}, bf16[256,1024]{1,0:T(8,128)(2,1)S(1)}, u32[]{:S(2)}, u32[]{:S(2)}) %collective-permute-start.4) | collective-permute-done | bytes 524320 | tf_op jit(solution)/shard_map/ppermute | solution.py:27
  96.3 8.9 %collective-permute-done.5 = bf16[256,1024]{1,0:T(8,128)(2,1)S(1)} collective-permute-done((bf16[256,1024]{1,0:T(8,128)(2,1)S(1)}, bf16[256,1024]{1,0:T(8,128)(2,1)S(1)}, u32[]{:S(2)}, u32[]{:S(2)}) %collective-permute-start.5) | collective-permute-done | bytes 524320 | tf_op jit(solution)/shard_map/ppermute | solution.py:27
  107.8 4.0 %fusion.72 = f32[1024,1024]{0,1:T(8,128)S(1)} fusion(bf16[1024,1024]{1,0:T(8,128)(2,1)} %bitcast.22, bf16[1024,1024]{1,0:T(8,128)(2,1)S(1)} %bitcast.224), kind=kOutput, calls=%fused_computation.79 | convolution fusion | flops 2147483648 | bytes 8388608 | tf_op jit(solution)/shard_map/dot_general | solution.py:182
  118.3 4.6 %all-to-all-start.1 = ((bf16[4,4,64,1024]{3,2,1,0:T(8,128)(2,1)}), bf16[4,4,64,1024]{3,2,1,0:T(8,128)(2,1)}, u32[]{:S(2)}, u32[]{:S(2)}) async-start(bf16[4,4,64,1024]{3,2,1,0:T(8,128)(2,1)} %maximum_bitcast_fusion), calls=%async_computation.4 | async-start | bytes 4194304 | tf_op jit(solution)/shard_map/all_to_all | solution.py:38
  123.7 19.6 %all-to-all-done.1 = bf16[4,4,64,1024]{3,2,1,0:T(8,128)(2,1)} async-done(((bf16[4,4,64,1024]{3,2,1,0:T(8,128)(2,1)}), bf16[4,4,64,1024]{3,2,1,0:T(8,128)(2,1)}, u32[]{:S(2)}, u32[]{:S(2)}) %all-to-all-start.1) | async-done | bytes 2097184 | tf_op jit(solution)/shard_map/all_to_all | solution.py:38
  143.2 18.6 %all-to-all-start = ((s32[128,64,1]{0,2,1:T(1,128)}), s32[128,64,1]{0,2,1:T(1,128)S(1)}, u32[]{:S(2)}, u32[]{:S(2)}) async-start(s32[128,64,1]{0,2,1:T(1,128)} %bitcast.30), calls=%async_computation.3 | async-start | bytes 65536 | tf_op jit(solution)/shard_map/all_to_all | solution.py:174
  161.9 3.0 %reduce_sum.21 = bf16[4,64,1024]{2,1,0:T(8,128)(2,1)} reduce(bf16[4,4,64,1024]{3,2,1,0:T(8,128)(2,1)} %all-to-all-done.1, bf16[]{:T(256)} %constant.117.clone.1), dimensions={0}, to_apply=%region_3.4 | reduce | flops 786432 | bytes 2621442 | tf_op jit(solution)/shard_map/reduce_sum | solution.py:39
  168.0 5.3 %copy.26 = bf16[256,32,32]{1,2,0:T(8,128)(2,1)} copy(bf16[256,32,32]{0,2,1:T(8,128)(2,1)} %reshape_reshape.11) | data formatting | bytes 1048576 | tf_op jit(solution)/shard_map/reshape;reshape | solution.py:65
  178.9 10.5 %all-to-all-start.2 = ((bf16[128,64,128]{2,0,1:T(8,128)(2,1)}), bf16[128,64,128]{2,0,1:T(8,128)(2,1)}, u32[]{:S(2)}, u32[]{:S(2)}) async-start(bf16[128,64,128]{2,0,1:T(8,128)(2,1)} %bitcast.215), calls=%async_computation.5 | async-start | bytes 4194304 | tf_op jit(solution)/shard_map/all_to_all | solution.py:173
  190.4 50.1 %all-to-all-done.2 = bf16[128,64,128]{2,0,1:T(8,128)(2,1)} async-done(((bf16[128,64,128]{2,0,1:T(8,128)(2,1)}), bf16[128,64,128]{2,0,1:T(8,128)(2,1)}, u32[]{:S(2)}, u32[]{:S(2)}) %all-to-all-start.2) | async-done | bytes 2097184 | tf_op jit(solution)/shard_map/all_to_all | solution.py:173
  240.5 15.5 %while.11 = (s32[]{:T(128)}, f32[1,1024,128]{2,1,0:T(8,128)S(1)}, s32[4,2048,1]{1,2,0:T(1,128)S(1)}, bf16[4,2048,1,128]{3,1,2,0:T(8,128)(2,1)}, s32[]{:T(128)}, /*index=5*/s32[]{:T(128)}) while((s32[]{:T(128)}, f32[1,1024,128]{2,1,0:T(8,128)S(1)}, s32[4,2048,1]{1,2,0:T(1,128)S(1)}, bf16[4,2048,1,128]{3,1,2,0:T(8,128)(2,1)}, ...), condition=%wide.region_5.6_spmd.clone, body=%wide.region_4.5_spmd.clone.sunk | while | flops 539230208 | bytes 1598035 | solution.py:101
  240.5 3.8 %fusion.91 = f32[1,1024,128]{2,1,0:T(8,128)S(1)} fusion(s32[2048]{0:T(1024)S(1)} %bitcast.222, f32[1,1024,128]{2,1,0:T(8,128)S(1)} %get-tuple-element.113, bf16[4,2048,1,128]{3,1,2,0:T(8,128)(2,1)} %get-tuple-element.121, s32[]{:T(128)} %get-tuple-element.112, pred[]{:T(512)S(6)} %compare.5), kind=kOutput, calls=%fused_computation.6.clone.1 | convolution fusion | flops 539230208 | bytes 1581569 | tf_op jit(solution)/shard_map/while/body/eval_jaxpr/qsr,qse->sre/dot_general | solution.py:96
  244.4 3.8 %fusion.91 = f32[1,1024,128]{2,1,0:T(8,128)S(1)} fusion(s32[2048]{0:T(1024)S(1)} %bitcast.222, f32[1,1024,128]{2,1,0:T(8,128)S(1)} %get-tuple-element.113, bf16[4,2048,1,128]{3,1,2,0:T(8,128)(2,1)} %get-tuple-element.121, s32[]{:T(128)} %get-tuple-element.112, pred[]{:T(512)S(6)} %compare.5), kind=kOutput, calls=%fused_computation.6.clone.1 | convolution fusion | flops 539230208 | bytes 1581569 | tf_op jit(solution)/shard_map/while/body/eval_jaxpr/qsr,qse->sre/dot_general | solution.py:96
  248.3 3.8 %fusion.91 = f32[1,1024,128]{2,1,0:T(8,128)S(1)} fusion(s32[2048]{0:T(1024)S(1)} %bitcast.222, f32[1,1024,128]{2,1,0:T(8,128)S(1)} %get-tuple-element.113, bf16[4,2048,1,128]{3,1,2,0:T(8,128)(2,1)} %get-tuple-element.121, s32[]{:T(128)} %get-tuple-element.112, pred[]{:T(512)S(6)} %compare.5), kind=kOutput, calls=%fused_computation.6.clone.1 | convolution fusion | flops 539230208 | bytes 1581569 | tf_op jit(solution)/shard_map/while/body/eval_jaxpr/qsr,qse->sre/dot_general | solution.py:96
  252.2 3.8 %fusion.91 = f32[1,1024,128]{2,1,0:T(8,128)S(1)} fusion(s32[2048]{0:T(1024)S(1)} %bitcast.222, f32[1,1024,128]{2,1,0:T(8,128)S(1)} %get-tuple-element.113, bf16[4,2048,1,128]{3,1,2,0:T(8,128)(2,1)} %get-tuple-element.121, s32[]{:T(128)} %get-tuple-element.112, pred[]{:T(512)S(6)} %compare.5), kind=kOutput, calls=%fused_computation.6.clone.1 | convolution fusion | flops 539230208 | bytes 1581569 | tf_op jit(solution)/shard_map/while/body/eval_jaxpr/qsr,qse->sre/dot_general | solution.py:96
  257.8 8.8 %all_to_all.41 = f32[4,1,128,128]{3,2,1,0:T(8,128)S(1)} all-to-all(f32[4,1,128,128]{3,2,1,0:T(8,128)S(1)} %bitcast.217), channel_id=1, replica_groups=mesh['section'=4,'owner_0'=4,'owner_1'=8,'owner_2'=2] {'section'}, dimensions={0} | all-to-all | bytes 524288 | tf_op jit(solution)/shard_map/all_to_all | solution.py:44
  267.2 16.5 %reduce-scatter.8.cloned.1.call-done = f32[1,16,1024]{2,1,0:T(8,128)} async-done(((f32[8,16,1024]{2,1,0:T(8,128)}), f32[1,16,1024]{2,1,0:T(8,128)}) %reduce-scatter.8.cloned.1.call-update) | async-done | bytes 65552 | tf_op jit(solution)/shard_map/reduce_scatter | solution.py:54
  (74 shorter events, 49.8 us)
Async XLA Ops:
  7.2 166.2 %copy-start = (bf16[4,64,32,128]{3,2,1,0:T(8,128)(2,1)S(1)}, bf16[4,64,32,128]{3,2,1,0:T(8,128)(2,1)}, u32[]{:S(2)}) copy-start(bf16[4,64,32,128]{3,2,1,0:T(8,128)(2,1)} %param.12) | copy-start | bytes 6291460
  7.2 182.3 %reduce-scatter.4.cloned.1.call-start = ((), (), s32[]{:S(2)}) async-start(), calls=%async_computation.7 | async-start | bytes 6291456 | tf_op jit(solution)/shard_map/reduce_scatter | solution.py:54
  10.1 13.5 %collective-permute-start = (bf16[256,1024]{1,0:T(8,128)(2,1)S(1)}, bf16[256,1024]{1,0:T(8,128)(2,1)S(1)}, u32[]{:S(2)}, u32[]{:S(2)}) collective-permute-start(bf16[256,1024]{1,0:T(8,128)(2,1)S(1)} %fusion.29), channel_id=1, source_target_pairs={{64,0},{128,64},{192,128},{65,1},{129,65},{193,129},{66,2},{130,66... | collective-permute-start | bytes 1572872 | tf_op jit(solution)/shard_map/ppermute | solution.py:27
  13.8 12.3 %copy-start.8 = (bf16[1,1024,1024]{2,1,0:T(8,128)(2,1)S(1)}, bf16[1,1024,1024]{2,1,0:T(8,128)(2,1)}, u32[]{:S(2)}) copy-start(bf16[1,1024,1024]{2,1,0:T(8,128)(2,1)} %param.8) | copy-start | bytes 6291460
  26.8 15.7 %collective-permute-start.1 = (bf16[256,1024]{1,0:T(8,128)(2,1)S(1)}, bf16[256,1024]{1,0:T(8,128)(2,1)S(1)}, u32[]{:S(2)}, u32[]{:S(2)}) collective-permute-start(bf16[256,1024]{1,0:T(8,128)(2,1)S(1)} %fusion.32), channel_id=1, source_target_pairs={{64,0},{128,64},{192,128},{65,1},{129,65},{193,129},{66,2},{130,66... | collective-permute-start | bytes 1572872 | tf_op jit(solution)/shard_map/ppermute | solution.py:27
  28.1 17.0 %copy-start.9 = (bf16[1,1024,1024]{2,1,0:T(8,128)(2,1)S(1)}, bf16[1,1024,1024]{2,1,0:T(8,128)(2,1)}, u32[]{:S(2)}) copy-start(bf16[1,1024,1024]{2,1,0:T(8,128)(2,1)} %param.8) | copy-start | bytes 6291460
  45.9 13.0 %collective-permute-start.2 = (bf16[256,1024]{1,0:T(8,128)(2,1)S(1)}, bf16[256,1024]{1,0:T(8,128)(2,1)S(1)}, u32[]{:S(2)}, u32[]{:S(2)}) collective-permute-start(bf16[256,1024]{1,0:T(8,128)(2,1)S(1)} %fusion.35), channel_id=1, source_target_pairs={{64,0},{128,64},{192,128},{65,1},{129,65},{193,129},{66,2},{130,66... | collective-permute-start | bytes 1572872 | tf_op jit(solution)/shard_map/ppermute | solution.py:27
  47.2 14.3 %copy-start.10 = (bf16[1,1024,1024]{2,1,0:T(8,128)(2,1)S(1)}, bf16[1,1024,1024]{2,1,0:T(8,128)(2,1)}, u32[]{:S(2)}) copy-start(bf16[1,1024,1024]{2,1,0:T(8,128)(2,1)} %param.8) | copy-start | bytes 6291460
  63.1 12.1 %collective-permute-start.3 = (bf16[256,1024]{1,0:T(8,128)(2,1)S(1)}, bf16[256,1024]{1,0:T(8,128)(2,1)S(1)}, u32[]{:S(2)}, u32[]{:S(2)}) collective-permute-start(bf16[256,1024]{1,0:T(8,128)(2,1)S(1)} %get-tuple-element.80), channel_id=1, source_target_pairs={{64,0},{128,64},{192,128},{65,1},{129,65},{193,129},{66,2},{130,66... | collective-permute-start | bytes 1572872 | tf_op jit(solution)/shard_map/ppermute | solution.py:27
  64.4 13.4 %copy-start.11 = (bf16[1,1024,1024]{2,1,0:T(8,128)(2,1)S(1)}, bf16[1,1024,1024]{2,1,0:T(8,128)(2,1)}, u32[]{:S(2)}) copy-start(bf16[1,1024,1024]{2,1,0:T(8,128)(2,1)} %param.8) | copy-start | bytes 6291460
  79.3 11.3 %collective-permute-start.4 = (bf16[256,1024]{1,0:T(8,128)(2,1)S(1)}, bf16[256,1024]{1,0:T(8,128)(2,1)S(1)}, u32[]{:S(2)}, u32[]{:S(2)}) collective-permute-start(bf16[256,1024]{1,0:T(8,128)(2,1)S(1)} %get-tuple-element.78), channel_id=1, source_target_pairs={{64,0},{128,64},{192,128},{65,1},{129,65},{193,129},{66,2},{130,66... | collective-permute-start | bytes 1572872 | tf_op jit(solution)/shard_map/ppermute | solution.py:27
  80.6 12.6 %copy-start.12 = (bf16[1,1024,1024]{2,1,0:T(8,128)(2,1)S(1)}, bf16[1,1024,1024]{2,1,0:T(8,128)(2,1)}, u32[]{:S(2)}) copy-start(bf16[1,1024,1024]{2,1,0:T(8,128)(2,1)} %param.8) | copy-start | bytes 6291460
  94.8 10.4 %collective-permute-start.5 = (bf16[256,1024]{1,0:T(8,128)(2,1)S(1)}, bf16[256,1024]{1,0:T(8,128)(2,1)S(1)}, u32[]{:S(2)}, u32[]{:S(2)}) collective-permute-start(bf16[256,1024]{1,0:T(8,128)(2,1)S(1)} %get-tuple-element.76), channel_id=1, source_target_pairs={{64,0},{128,64},{192,128},{65,1},{129,65},{193,129},{66,2},{130,66... | collective-permute-start | bytes 1572872 | tf_op jit(solution)/shard_map/ppermute | solution.py:27
  96.3 11.5 %copy-start.7 = (bf16[1,4,256,1024]{3,2,1,0:T(8,128)(2,1)S(1)}, bf16[1,4,256,1024]{3,2,1,0:T(8,128)(2,1)}, u32[]{:S(2)}) copy-start(bf16[1,4,256,1024]{3,2,1,0:T(8,128)(2,1)} %param.9) | copy-start | bytes 6291460
  114.1 2.5 copy-start.3
  114.1 2.5 copy-start.4
  118.3 4.6 %copy-start.6 = (s32[4,64,32]{1,2,0:T(8,128)S(1)}, s32[4,64,32]{1,2,0:T(8,128)}, u32[]{:S(2)}) copy-start(s32[4,64,32]{1,2,0:T(8,128)} %param.13) | copy-start | bytes 98308
  118.3 24.9 %all-to-all-start.1 = ((bf16[4,4,64,1024]{3,2,1,0:T(8,128)(2,1)}), bf16[4,4,64,1024]{3,2,1,0:T(8,128)(2,1)}, u32[]{:S(2)}, u32[]{:S(2)}) async-start(bf16[4,4,64,1024]{3,2,1,0:T(8,128)(2,1)} %maximum_bitcast_fusion), calls=%async_computation.4 | async-start | bytes 4194304 | tf_op jit(solution)/shard_map/all_to_all | solution.py:38
  143.2 35.7 %all-to-all-start = ((s32[128,64,1]{0,2,1:T(1,128)}), s32[128,64,1]{0,2,1:T(1,128)S(1)}, u32[]{:S(2)}, u32[]{:S(2)}) async-start(s32[128,64,1]{0,2,1:T(1,128)} %bitcast.30), calls=%async_computation.3 | async-start | bytes 65536 | tf_op jit(solution)/shard_map/all_to_all | solution.py:174
  173.4 2.6 copy-start.1
  178.9 61.6 %all-to-all-start.2 = ((bf16[128,64,128]{2,0,1:T(8,128)(2,1)}), bf16[128,64,128]{2,0,1:T(8,128)(2,1)}, u32[]{:S(2)}, u32[]{:S(2)}) async-start(bf16[128,64,128]{2,0,1:T(8,128)(2,1)} %bitcast.215), calls=%async_computation.5 | async-start | bytes 4194304 | tf_op jit(solution)/shard_map/all_to_all | solution.py:173
  189.4 66.6 %reduce-scatter.6.cloned.1.call-start = ((), (), s32[]{:S(2)}) async-start(), calls=%async_computation.8 | async-start | bytes 2621440 | tf_op jit(solution)/shard_map/reduce_scatter | solution.py:54
  190.2 93.6 %reduce-scatter.8.cloned.1.call-start = ((), (), s32[]{:S(2)}) async-start(), calls=%async_computation.9 | async-start | bytes 589824 | tf_op jit(solution)/shard_map/reduce_scatter | solution.py:54
  256.1 1.6 collective-permute-start.6
  (2 other events, 4.8 us)
Sparse Core Ops, SparseCore 0:
  114.2 26.3 reduce-scatter.3
  192.8 46.1 reduce-scatter.5
  256.2 27.5 reduce-scatter.7
where the time goes:
time: 297 us; the launch traced here: 292 us
  waiting for transfers between devices  151 us (51%)
  starting transfers between devices  42.5 us (14%)
  matrix products  34.1 us (11%)
  other arithmetic  24.7 us (8%)
  local copies, waits for them, and re-layouts  16.1 us (5%)
  between operations  14.1 us (5%)
  blocking collectives  8.78 us (3%)
    ppermute x6, waiting for transfers between devices, passed_along(): return lax.ppermute(x, axis, pairs)  63.2 us
    all_to_all x1, waiting for transfers between devices, per_device(): lax.all_to_all(outgoing, OWNER, split_axis=1, concat_axis=0, tiled=True)  50.1 us
    all_to_all x1, waiting for transfers between devices, sum_at_owner(): parts = lax.all_to_all(cut_along(x, dim, count), axis, 0, 0, tiled=True)  19.6 us
    all_to_all x1, starting transfers between devices, per_device(): lax.all_to_all(out_ids, OWNER, split_axis=1, concat_axis=0, tiled=True)  18.6 us
    select_n x7, other arithmetic, per_device(): jnp.where(active, lax.dynamic_update_index_in_dim(slopes, slope, clipped,...  17.9 us
    reduce_scatter x3, waiting for transfers between devices, sum_in_order(): parts = lax.psum_scatter(parts, axes[k], scatter_dimension=0, tiled=True)  16.6 us
    dot_general x4, matrix products, add_block(): jnp.einsum('qsr,qse->sre', onehot, pieces, preferred_element_type=jnp.flo...  15.4 us
    dot_general x7, matrix products, per_device(): lax.dot_general(slope, layer_w, (((1,), (1,)), ((), ())), preferred_eleme...  11.5 us
  transfers between devices with their start and end apart: 13, of which 10 were waited for; matrix products, arithmetic and copies ran while one was open for 14% of the time, Pallas kernels for 0%

commit v1 on v0

--- a/solution.py
+++ b/solution.py
@@ -1,8 +1,12 @@
 import math
+
+import functools
 
 import jax
 import jax.numpy as jnp
 from jax import lax
+from jax.experimental import pallas as pl
+from jax.experimental.pallas import tpu as pltpu
 from jax.sharding import Mesh
 from jax.sharding import PartitionSpec as P
 
@@ -115,6 +119,147 @@
     sending = jnp.where(upper_side, lower, upper)
     partial_value = kept + partner(sending, OWNER, 0)
     return partial_value
+
+
+def chain_kernel(
+    micros, sections,
+    w_hbm, pre_hbm, cot_hbm, slopes_out, p_out,
+    w_v, pre_v, rbuf, sbuf,
+    w_sem, pre_sem, in_sem, out_sem, p_recv, p_send,
+):
+    section = lax.axis_index("section")
+    chunks = micros * sections
+    rows = pre_v.shape[0] // chunks
+    last = section == sections - 1
+
+    def part(ref, t):
+        return ref.at[pl.ds(pl.multiple_of(t * rows, rows), rows)]
+
+    def pre_copy(t):
+        return pltpu.make_async_copy(part(pre_hbm, t), part(pre_v, t), pre_sem.at[t])
+
+    def cot_copy(t):
+        return pltpu.make_async_copy(part(cot_hbm, t), part(rbuf, t), in_sem.at[t])
+
+    def down_copy(t):
+        return pltpu.make_async_remote_copy(
+            src_ref=part(sbuf, t), dst_ref=part(rbuf, t),
+            send_sem=out_sem.at[t], recv_sem=in_sem.at[t],
+            device_id={"section": lax.rem(section + sections - 1, sections)},
+            device_id_type=pl.DeviceIdType.MESH,
+        )
+
+    def p_copy(t):
+        m = t // sections
+        return pltpu.make_async_remote_copy(
+            src_ref=part(sbuf, t), dst_ref=part(p_out, m),
+            send_sem=p_send.at[t], recv_sem=p_recv.at[m],
+            device_id={"section": lax.rem(t, sections)},
+            device_id_type=pl.DeviceIdType.MESH,
+        )
+
+    w_copy = pltpu.make_async_copy(w_hbm, w_v, w_sem)
+    w_copy.start()
+
+    def begin(t, carry):
+        pre_copy(t).start()
+
+        @pl.when(last)
+        def _():
+            cot_copy(t).start()
+        return carry
+
+    lax.fori_loop(0, chunks, begin, 0)
+    barrier = pltpu.get_barrier_semaphore()
+    for d in range(1, sections):
+        pl.semaphore_signal(
+            barrier, inc=1, device_id={"section": lax.rem(section + d, sections)},
+            device_id_type=pl.DeviceIdType.MESH,
+        )
+    pl.semaphore_wait(barrier, sections - 1)
+    w_copy.wait()
+
+    def step(t, carry):
+        pre_copy(t).wait()
+
+        @pl.when(last)
+        def _():
+            cot_copy(t).wait()
+
+        @pl.when(jnp.logical_not(last))
+        def _():
+            down_copy(t).wait_recv()
+
+        at = pl.ds(pl.multiple_of(t * rows, rows), rows)
+        incoming = rbuf[at, :]
+        slope = jnp.where(pre_v[at, :] > 0, incoming, jnp.zeros_like(incoming))
+        slopes_out[at, :] = slope
+        sbuf[at, :] = lax.dot_general(
+            slope, w_v[...], (((1,), (1,)), ((), ())), preferred_element_type=jnp.float32
+        ).astype(jnp.bfloat16)
+
+        @pl.when(section > 0)
+        def _():
+            down_copy(t).start()
+
+        @pl.when((section == 0) & (lax.rem(t, sections) > 0))
+        def _():
+            p_copy(t).start()
+
+        @pl.when((section == 0) & (lax.rem(t, sections) == 0))
+        def _():
+            own = pl.multiple_of((t // sections) * rows, rows)
+            p_out[pl.ds(own, rows), :] = sbuf[at, :]
+        return carry
+
+    lax.fori_loop(0, chunks, step, 0)
+
+    def finish(t, carry):
+        @pl.when(section > 0)
+        def _():
+            down_copy(t).wait_send()
+
+        @pl.when((section == 0) & (lax.rem(t, sections) > 0))
+        def _():
+            p_copy(t).wait_send()
+        return carry
+
+    lax.fori_loop(0, chunks, finish, 0)
+
+    @pl.when(section > 0)
+    def _():
+        def take(m, carry):
+            p_copy(m * sections).wait_recv()
+            return carry
+
+        lax.fori_loop(0, micros, take, 0)
+
+
+def chain(w, pre, cot, micros, sections):
+    total, hidden = pre.shape
+    chunks = micros * sections
+    dma = pltpu.SemaphoreType.DMA
+    vmem = pl.BlockSpec(memory_space=pltpu.VMEM)
+    hbm = pl.BlockSpec(memory_space=pl.ANY)
+    slopes, portion = pl.pallas_call(
+        functools.partial(chain_kernel, micros, sections),
+        out_shape=(
+            jax.ShapeDtypeStruct((total, hidden), jnp.bfloat16),
+            jax.ShapeDtypeStruct((total // sections, hidden), jnp.bfloat16),
+        ),
+        in_specs=[hbm] * 3,
+        out_specs=(vmem, vmem),
+        scratch_shapes=[
+            pltpu.VMEM((hidden, hidden), jnp.bfloat16),
+            pltpu.VMEM((total, hidden), jnp.bfloat16),
+            pltpu.VMEM((total, hidden), jnp.bfloat16),
+            pltpu.VMEM((total, hidden), jnp.bfloat16),
+            dma, dma((chunks,)), dma((chunks,)), dma((chunks,)), dma((micros,)), dma((chunks,)),
+        ],
+        compiler_params=pltpu.CompilerParams(collective_id=0, has_side_effects=True,
+                                             vmem_limit_bytes=32 * 1024 * 1024),
+    )(w, pre, cot)
+    return slopes, portion.reshape(micros, total // sections // micros, hidden)
 
 
 def per_device(weights, inputs, preact, cotangent, embeddings, row_ids):
@@ -127,40 +272,14 @@
     emb_width = embeddings.shape[3]
     row_split = max(1, owners // features)
     grad_scale = 1.0 / math.sqrt(micro_count * batch_rows * owners)
-    layer_w = weights[0]
     layer_in = inputs[0]
-    layer_pre = preact[0]
-    is_last = section_pos == sections - 1
-    received = jnp.zeros((batch_rows, hidden), jnp.bfloat16)
-    slopes = jnp.zeros((micro_count, batch_rows, hidden), jnp.bfloat16)
-    section_zero = []
-    row_table = 0.0
-    moments = micro_count + sections - 1
-    for moment in range(moments):
-        micro_pos = moment - (sections - 1 - section_pos)
-        active = (micro_pos >= 0) & (micro_pos < micro_count)
-        clipped = jnp.clip(micro_pos, 0, micro_count - 1)
-        fresh = lax.dynamic_index_in_dim(cotangent, clipped, 0, False)
-        incoming = jnp.where(is_last, fresh, received)
-        pre_now = lax.dynamic_index_in_dim(layer_pre, clipped, 0, False)
-        slope = jnp.where(active & (pre_now > 0), incoming, jnp.zeros_like(incoming))
-        slopes = jnp.where(
-            active, lax.dynamic_update_index_in_dim(slopes, slope, clipped, 0), slopes
-        )
-        passed = lax.dot_general(
-            slope, layer_w, (((1,), (1,)), ((), ())), preferred_element_type=jnp.float32
-        ).astype(jnp.bfloat16)
-        if moment >= sections - 1:
-            from_zero = jnp.where(
-                section_pos == 0,
-                passed.astype(jnp.float32),
-                jnp.zeros((batch_rows, hidden), jnp.float32),
-            )
-            section_zero.append(from_zero)
-        if moment + 1 < moments:
-            received = passed_along(passed, "section", -1)
-    stacked = jnp.stack(section_zero)
-    portion = sum_at_owner(stacked.astype(jnp.bfloat16), "section", 1).astype(jnp.bfloat16)
+    slopes, portion = chain(
+        weights[0],
+        preact.reshape(micro_count * batch_rows, hidden),
+        cotangent.reshape(micro_count * batch_rows, hidden),
+        micro_count,
+        sections,
+    )
     quarter = portion.shape[1]
     feat_grads = pair_grads(
         portion.reshape(micro_count * quarter, hidden),

time: 297 us -> 231 us (0.78)
  the two profiles are of different devices: /device:TPU:1 before, /device:TPU:8 now
where the time goes in v1:
time: 231 us; the launch traced here: 230 us
  waiting for transfers between devices  74.4 us (32%)
  Pallas kernels  66.4 us (29%)
  starting transfers between devices  23.1 us (10%)
  matrix products  21.1 us (9%)
  local copies, waits for them, and re-layouts  15.1 us (7%)
  between operations  13.9 us (6%)
  blocking collectives  13.8 us (6%)
    pallas_call x1, Pallas kernels, chain(): pl.pallas_call(functools.partial(chain_kernel, micros, sections), out_sha...  66.4 us
    all_to_all x1, waiting for transfers between devices, per_device(): lax.all_to_all(outgoing, OWNER, split_axis=1, concat_axis=0, tiled=True)  50 us
    reduce_scatter x3, waiting for transfers between devices, sum_in_order(): parts = lax.psum_scatter(parts, axes[k], scatter_dimension=0, tiled=True)  22.3 us
    dot_general x4, matrix products, add_block(): jnp.einsum('qsr,qse->sre', onehot, pieces, preferred_element_type=jnp.flo...  15.4 us
    all_to_all x1, blocking collectives, summed_on_arrival(): parts = lax.all_to_all(cut_along(x, dim, count), axis, 0, 0, tiled=True)  13.8 us
    all_to_all x1, starting transfers between devices, per_device(): lax.all_to_all(out_ids, OWNER, split_axis=1, concat_axis=0, tiled=True)  11.9 us
    all_to_all x1, starting transfers between devices, per_device(): lax.all_to_all(outgoing, OWNER, split_axis=1, concat_axis=0, tiled=True)  10.7 us
    unnamed x15, local copies, waits for them, and re-layouts  5.78 us
  transfers between devices with their start and end apart: 6, of which 3 were waited for; matrix products, arithmetic and copies ran while one was open for 12% of the time, Pallas kernels for 0%

profile of v1, /device:TPU:8, one launch (start us, length us, event | category | flops | bytes accessed | tf_op | source)
XLA Modules:
  0.0 230.2 jit_solution(11903912439747146388)
XLA Ops:
  7.2 1.7 copy-done.1
  9.0 1.6 copy-done.2
  10.6 1.6 copy-done.3
  12.1 66.4 %shard_map.77 = (bf16[1024,1024]{1,0:T(8,128)(2,1)S(1)}, bf16[256,1024]{1,0:T(8,128)(2,1)S(1)}) custom-call(bf16[1024,1024]{1,0:T(8,128)(2,1)S(1)} %bitcast.67, bf16[1024,1024]{1,0:T(8,128)(2,1)S(1)} %bitcast.68, bf16[1024,1024]{1,0:T(8,128)(2,1)S(1)} %bitcast.69), custom_call_target="tpu_custom_call" | custom-call | tf_op jit(solution)/shard_map/pallas_call | solution.py:244
  78.5 2.4 %fusion.15 = f32[1024,1024]{0,1:T(8,128)S(1)} fusion(bf16[1024,1024]{1,0:T(8,128)(2,1)S(1)} %get-tuple-element.31, bf16[1024,1024]{1,0:T(8,128)(2,1)S(1)} %bitcast.78), kind=kOutput, calls=%fused_computation.16 | convolution fusion | flops 2147483648 | bytes 8388608 | tf_op jit(solution)/shard_map/dot_general | solution.py:301
  80.9 2.3 copy.17
  83.2 0.8 copy-done.5
  84.1 0.7 reshape_reshape.7
  84.8 11.9 %all-to-all-start = ((s32[128,64,1]{0,2,1:T(1,128)}), s32[128,64,1]{0,2,1:T(1,128)S(1)}, u32[]{:S(2)}, u32[]{:S(2)}) async-start(s32[128,64,1]{0,2,1:T(1,128)} %bitcast.10), calls=%async_computation.3 | async-start | bytes 65536 | tf_op jit(solution)/shard_map/all_to_all | solution.py:293
  97.0 4.0 %copy.22 = bf16[256,32,32]{1,2,0:T(8,128)(2,1)} copy(bf16[256,32,32]{0,2,1:T(8,128)(2,1)S(1)} %bitcast.74) | data formatting | bytes 1048576 | tf_op jit(solution)/shard_map/reshape;reshape;reshape | solution.py:69
  100.9 2.7 %fusion.16 = f32[256,32,128]{2,1,0:T(8,128)S(1)} fusion(bf16[256,32,32]{1,2,0:T(8,128)(2,1)} %copy.22, bf16[256,32,128]{2,1,0:T(8,128)(2,1)S(1)} %bitcast.65), kind=kOutput, calls=%fused_computation.17 | convolution fusion | flops 67108864 | bytes 6815744 | tf_op jit(solution)/shard_map/qfg,qge->qfe/dot_general | solution.py:70
  103.6 0.7 add_convert_fusion
  104.3 2.2 copy.23
  106.5 10.7 %all-to-all-start.1 = ((bf16[128,64,128]{2,0,1:T(8,128)(2,1)}), bf16[128,64,128]{2,0,1:T(8,128)(2,1)}, u32[]{:S(2)}, u32[]{:S(2)}) async-start(bf16[128,64,128]{2,0,1:T(8,128)(2,1)} %bitcast.72), calls=%async_computation.4 | async-start | bytes 4194304 | tf_op jit(solution)/shard_map/all_to_all | solution.py:292
  118.2 50.0 %all-to-all-done.1 = bf16[128,64,128]{2,0,1:T(8,128)(2,1)} async-done(((bf16[128,64,128]{2,0,1:T(8,128)(2,1)}), bf16[128,64,128]{2,0,1:T(8,128)(2,1)}, u32[]{:S(2)}, u32[]{:S(2)}) %all-to-all-start.1) | async-done | bytes 2097184 | tf_op jit(solution)/shard_map/all_to_all | solution.py:292
  168.2 15.5 %while.11 = (s32[]{:T(128)}, f32[1,1024,128]{2,1,0:T(8,128)S(1)}, s32[4,2048,1]{1,2,0:T(1,128)S(1)}, bf16[4,2048,1,128]{3,1,2,0:T(8,128)(2,1)}, s32[]{:T(128)}, /*index=5*/s32[]{:T(128)}) while((s32[]{:T(128)}, f32[1,1024,128]{2,1,0:T(8,128)S(1)}, s32[4,2048,1]{1,2,0:T(1,128)S(1)}, bf16[4,2048,1,128]{3,1,2,0:T(8,128)(2,1)}, ...), condition=%wide.region_4.5_spmd.clone, body=%wide.region_3.4_spmd.clone.sunk | while | flops 539230208 | bytes 1597535 | solution.py:105
  168.2 3.8 %fusion.28 = f32[1,1024,128]{2,1,0:T(8,128)S(1)} fusion(s32[2048]{0:T(1024)S(1)} %bitcast.76, f32[1,1024,128]{2,1,0:T(8,128)S(1)} %get-tuple-element.99, bf16[4,2048,1,128]{3,1,2,0:T(8,128)(2,1)} %get-tuple-element.107, s32[]{:T(128)S(6)} %copy.28, pred[]{:T(512)S(6)} %compare.5), kind=kOutput, calls=%fused_computation.6.clone.1 | convolution fusion | flops 539230208 | bytes 1581061 | tf_op jit(solution)/shard_map/while/body/eval_jaxpr/qsr,qse->sre/dot_general | solution.py:100
  172.1 3.8 %fusion.28 = f32[1,1024,128]{2,1,0:T(8,128)S(1)} fusion(s32[2048]{0:T(1024)S(1)} %bitcast.76, f32[1,1024,128]{2,1,0:T(8,128)S(1)} %get-tuple-element.99, bf16[4,2048,1,128]{3,1,2,0:T(8,128)(2,1)} %get-tuple-element.107, s32[]{:T(128)S(6)} %copy.28, pred[]{:T(512)S(6)} %compare.5), kind=kOutput, calls=%fused_computation.6.clone.1 | convolution fusion | flops 539230208 | bytes 1581061 | tf_op jit(solution)/shard_map/while/body/eval_jaxpr/qsr,qse->sre/dot_general | solution.py:100
  176.0 3.8 %fusion.28 = f32[1,1024,128]{2,1,0:T(8,128)S(1)} fusion(s32[2048]{0:T(1024)S(1)} %bitcast.76, f32[1,1024,128]{2,1,0:T(8,128)S(1)} %get-tuple-element.99, bf16[4,2048,1,128]{3,1,2,0:T(8,128)(2,1)} %get-tuple-element.107, s32[]{:T(128)S(6)} %copy.28, pred[]{:T(512)S(6)} %compare.5), kind=kOutput, calls=%fused_computation.6.clone.1 | convolution fusion | flops 539230208 | bytes 1581061 | tf_op jit(solution)/shard_map/while/body/eval_jaxpr/qsr,qse->sre/dot_general | solution.py:100
  179.8 3.8 %fusion.28 = f32[1,1024,128]{2,1,0:T(8,128)S(1)} fusion(s32[2048]{0:T(1024)S(1)} %bitcast.76, f32[1,1024,128]{2,1,0:T(8,128)S(1)} %get-tuple-element.99, bf16[4,2048,1,128]{3,1,2,0:T(8,128)(2,1)} %get-tuple-element.107, s32[]{:T(128)S(6)} %copy.28, pred[]{:T(512)S(6)} %compare.5), kind=kOutput, calls=%fused_computation.6.clone.1 | convolution fusion | flops 539230208 | bytes 1581061 | tf_op jit(solution)/shard_map/while/body/eval_jaxpr/qsr,qse->sre/dot_general | solution.py:100
  184.0 1.4 collective-permute-done
  185.5 13.8 %all_to_all.36 = f32[4,1,128,128]{3,2,1,0:T(8,128)S(1)} all-to-all(f32[4,1,128,128]{3,2,1,0:T(8,128)S(1)} %bitcast.75), channel_id=1, replica_groups=mesh['section'=4,'owner_0'=4,'owner_1'=8,'owner_2'=2] {'section'}, dimensions={0} | all-to-all | bytes 524288 | tf_op jit(solution)/shard_map/all_to_all | solution.py:48
  200.0 22.2 %reduce-scatter.8.cloned.1.call-done = f32[1,16,1024]{2,1,0:T(8,128)} async-done(((f32[8,16,1024]{2,1,0:T(8,128)}), f32[1,16,1024]{2,1,0:T(8,128)}) %reduce-scatter.8.cloned.1.call-update) | async-done | bytes 65552 | tf_op jit(solution)/shard_map/reduce_scatter | solution.py:58
  222.2 1.5 broadcast_multiply_fusion
  (31 shorter events, 2.3 us)
Async XLA Ops:
  7.2 93.7 %copy-start = (bf16[4,64,32,128]{3,2,1,0:T(8,128)(2,1)S(1)}, bf16[4,64,32,128]{3,2,1,0:T(8,128)(2,1)}, u32[]{:S(2)}) copy-start(bf16[4,64,32,128]{3,2,1,0:T(8,128)(2,1)} %param.12) | copy-start | bytes 6291460
  7.2 110.1 %reduce-scatter.4.cloned.1.call-start = ((), (), s32[]{:S(2)}) async-start(), calls=%async_computation.6 | async-start | bytes 6291456 | tf_op jit(solution)/shard_map/reduce_scatter | solution.py:58
  7.2 1.7 copy-start.1
  9.0 1.6 copy-start.2
  10.5 1.6 copy-start.3
  12.1 66.4 %copy-start.6 = (bf16[1,4,256,1024]{3,2,1,0:T(8,128)(2,1)S(1)}, bf16[1,4,256,1024]{3,2,1,0:T(8,128)(2,1)}, u32[]{:S(2)}) copy-start(bf16[1,4,256,1024]{3,2,1,0:T(8,128)(2,1)} %param.9) | copy-start | bytes 6291460
  83.2 0.8 copy-start.5
  84.8 21.7 %all-to-all-start = ((s32[128,64,1]{0,2,1:T(1,128)}), s32[128,64,1]{0,2,1:T(1,128)S(1)}, u32[]{:S(2)}, u32[]{:S(2)}) async-start(s32[128,64,1]{0,2,1:T(1,128)} %bitcast.10), calls=%async_computation.3 | async-start | bytes 65536 | tf_op jit(solution)/shard_map/all_to_all | solution.py:293
  100.9 2.7 %copy-start.4 = (bf16[256,32,32]{1,2,0:T(8,128)(2,1)S(1)}, bf16[256,32,32]{1,2,0:T(8,128)(2,1)}, u32[]{:S(2)}) copy-start(bf16[256,32,32]{1,2,0:T(8,128)(2,1)} %copy.22) | copy-start | bytes 1572868
  106.5 61.7 %all-to-all-start.1 = ((bf16[128,64,128]{2,0,1:T(8,128)(2,1)}), bf16[128,64,128]{2,0,1:T(8,128)(2,1)}, u32[]{:S(2)}, u32[]{:S(2)}) async-start(bf16[128,64,128]{2,0,1:T(8,128)(2,1)} %bitcast.72), calls=%async_computation.4 | async-start | bytes 4194304 | tf_op jit(solution)/shard_map/all_to_all | solution.py:292
  117.2 66.5 %reduce-scatter.6.cloned.1.call-start = ((), (), s32[]{:S(2)}) async-start(), calls=%async_computation.7 | async-start | bytes 2621440 | tf_op jit(solution)/shard_map/reduce_scatter | solution.py:58
  118.0 104.2 %reduce-scatter.8.cloned.1.call-start = ((), (), s32[]{:S(2)}) async-start(), calls=%async_computation.8 | async-start | bytes 589824 | tf_op jit(solution)/shard_map/reduce_scatter | solution.py:58
  183.8 1.6 collective-permute-start
Sparse Core Ops, SparseCore 0:
  83.3 24.0 reduce-scatter.3
  120.6 50.3 reduce-scatter.5
  183.9 38.2 reduce-scatter.7

commit v2 on v1

v2 whole, which is shorter than its diff:
```python
import functools
import math

import jax
import jax.numpy as jnp
from jax import lax
from jax.experimental import pallas as pl
from jax.experimental.pallas import tpu as pltpu
from jax.sharding import Mesh
from jax.sharding import PartitionSpec as P

OWNER = ("owner_0", "owner_1", "owner_2")
OWNER_SECTION = ("owner_0", "owner_1", "owner_2", "section")
MESH = pl.DeviceIdType.MESH
BF16 = jnp.bfloat16
F32 = jnp.float32
NN = (((1,), (0,)), ((), ()))
NT = (((1,), (1,)), ((), ()))
TN = (((0,), (0,)), ((), ()))
GROUP = 16


def dot(a, b, dims):
    return lax.dot_general(a, b, dims, preferred_element_type=F32)


def step_kernel(
    dims, scale,
    w_hbm, x_hbm, pre_hbm, cot_hbm, emb_hbm, ids_hbm,
    wg_out, tg_out,
    w_v, x_v, pre_v, emb_v, ids_v, rbuf, sbuf, slopes, pbuf, wacc, wrecv, wx, wxr, wz, wzr,
    fold, pick, spread, fg, arr, idr, onehot, acc, sib, yrecv,
    w_sem, x_sem, pre_sem, emb_sem, ids_sem, in_sem, out_sem, p_recv, p_send,
    id_send, id_recv, f_send, f_recv, ac_send, ac_recv, bx_send, bx_recv, cz_send, cz_recv,
    sib_send, sib_recv, y_send, y_recv,
):
    micros, sections, nx, nz, features = dims
    section = lax.axis_index("section")
    px = lax.axis_index("owner_0")
    pz = lax.axis_index("owner_1")
    pc = lax.axis_index("owner_2")
    chunks = micros * sections
    rows = pre_v.shape[0] // chunks
    hidden = w_v.shape[0]
    lanes = emb_v.shape[1]
    last = section == sections - 1

    def part(ref, t, size):
        return ref.at[pl.ds(pl.multiple_of(t * size, size), size)]

    def pre_copy(t):
        return pltpu.make_async_copy(part(pre_hbm, t, rows), part(pre_v, t, rows), pre_sem.at[t])

    def cot_copy(t):
        return pltpu.make_async_copy(part(cot_hbm, t, rows), part(rbuf, t, rows), in_sem.at[t])

    def remote(src, dst, send, recv, where):
        return pltpu.make_async_remote_copy(
            src_ref=src, dst_ref=dst, send_sem=send, recv_sem=recv,
            device_id=where, device_id_type=MESH,
        )

    def down_copy(t):
        return remote(
            part(sbuf, t, rows), part(rbuf, t, rows), out_sem.at[t], in_sem.at[t],
            {"section": lax.rem(section + sections - 1, sections)},
        )

    def p_copy(t):
        return remote(
            part(sbuf, t, rows), part(pbuf, t // sections, rows),
            p_send.at[t], p_recv.at[t // sections], {"section": lax.rem(t, sections)},
        )

    def chip(n):
        dx = lax.rem(n, nx)
        k = n // nx
        dz = ((k + 1) // 2) * (2 * lax.rem(k, 2) - 1)
        return lax.rem(px + dx, nx), lax.rem(pz + dz + nz, nz)

    w_copy = pltpu.make_async_copy(w_hbm, w_v, w_sem)
    x_copy = pltpu.make_async_copy(x_hbm, x_v, x_sem)
    emb_copy = pltpu.make_async_copy(emb_hbm, emb_v, emb_sem)
    ids_copy = pltpu.make_async_copy(ids_hbm, ids_v, ids_sem)
    w_copy.start()

    def begin(t, carry):
        pre_copy(t).start()

        @pl.when(last)
        def _():
            cot_copy(t).start()
        return carry

    lax.fori_loop(0, chunks, begin, 0)
    ids_copy.start()
    emb_copy.start()
    x_copy.start()

    barrier = pltpu.get_barrier_semaphore()
    for d in range(1, sections):
        pl.semaphore_signal(
            barrier, inc=1, device_id={"section": lax.rem(section + d, sections)},
            device_id_type=MESH,
        )

    def greet(n, carry):
        tx, tz = chip(n)

        def hail(core):
            pl.semaphore_signal(
                barrier, inc=1, device_id={"owner_0": tx, "owner_1": tz, "owner_2": core},
                device_id_type=MESH,
            )

        hail(1 - pc)

        @pl.when(n > 0)
        def _():
            hail(pc)
        return carry

    lax.fori_loop(0, nx * nz, greet, 0)

    across = lax.broadcasted_iota(jnp.int32, (128, hidden), 1)
    flipped = lax.rem(across, features) * features + across // features

    def make_fold(b, carry):
        down = lax.broadcasted_iota(jnp.int32, (128, hidden), 0) + b * 128
        value = jnp.where(down == across, 1.0, 0.0) + jnp.where(down == flipped, 1.0, 0.0)
        part(fold, b, 128)[...] = value.astype(BF16)
        return carry

    lax.fori_loop(0, hidden // 128, make_fold, 0)
    wide = GROUP * features
    for j in range(128 // features):
        down = lax.broadcasted_iota(jnp.int32, (128, wide), 0)
        col = lax.rem(lax.broadcasted_iota(jnp.int32, (128, wide), 1), features) + j * features
        pick[j] = jnp.where(down == col, 1.0, 0.0).astype(BF16)
    acc[...] = jnp.zeros_like(acc)

    pl.semaphore_wait(barrier, sections - 1 + 2 * nx * nz - 1)
    ids_copy.wait()

    def send_ids(n, carry):
        tx, tz = chip(n)
        mine = (px * nz + pz) * 2 + pc
        for r in range(2):
            there = (tx * nz + tz) * 2 + r
            home = (n == 0) & (pc == r)

            @pl.when(home)
            def _():
                pltpu.make_async_copy(ids_v.at[there], idr.at[mine], id_recv).start()

            @pl.when(jnp.logical_not(home))
            def _():
                remote(
                    ids_v.at[there], idr.at[mine], id_send, id_recv,
                    {"owner_0": tx, "owner_1": tz, "owner_2": r},
                ).start()
        return carry

    lax.fori_loop(0, nx * nz, send_ids, 0)
    w_copy.wait()

    def chain_step(t):
        pre_copy(t).wait()

        @pl.when(last)
        def _():
            cot_copy(t).wait()

        @pl.when(jnp.logical_not(last))
        def _():
            down_copy(t).wait_recv()

        at = pl.ds(pl.multiple_of(t * rows, rows), rows)
        incoming = rbuf[at, :]
        slope = jnp.where(pre_v[at, :] > 0, incoming, jnp.zeros_like(incoming))
        slopes[at, :] = slope
        sbuf[at, :] = dot(slope, w_v[...], NT).astype(BF16)

        @pl.when(section > 0)
        def _():
            down_copy(t).start()

        @pl.when((section == 0) & (lax.rem(t, sections) > 0))
        def _():
            p_copy(t).start()

        @pl.when((section == 0) & (lax.rem(t, sections) == 0))
        def _():
            own = pl.multiple_of((t // sections) * rows, rows)
            pbuf[pl.ds(own, rows), :] = sbuf[at, :]

    block = 256

    def weight_step(m):
        size = rows * sections
        at = pl.ds(pl.multiple_of(m * size, size), size)

        def column(b, carry):
            cols = pl.ds(pl.multiple_of(b * block, block), block)
            grown = dot(x_v[at, cols], slopes[at, :], TN)
            spot = pl.ds(b * (block // 32), block // 32)
            grown = grown.reshape(block // 32, 2, 16, hidden)

            @pl.when(m == 0)
            def _():
                wacc[spot] = grown

            @pl.when(m > 0)
            def _():
                wacc[spot] = wacc[spot] + grown
            return carry

        lax.fori_loop(0, hidden // block, column, 0)

    sibling = {"owner_2": 1 - pc}
    core_copy = remote(wacc.at[:, 1 - pc], wrecv, ac_send, ac_recv, sibling)

    def x_send(d):
        to = lax.rem(px + d, nx)
        return remote(part(wx, to, nz), wxr.at[d - 1], bx_send.at[d - 1], bx_recv.at[d - 1],
                      {"owner_0": to})

    def z_send(d):
        to = lax.rem(pz + d, nz)
        return remote(wz.at[to], wzr.at[d - 1], cz_send.at[d - 1], cz_recv.at[d - 1],
                      {"owner_1": to})

    def weight_x():
        core_copy.wait_recv()

        def join(k, carry):
            wx[k] = (wacc[k, pc] + wrecv[k]).astype(BF16)
            return carry

        lax.fori_loop(0, nx * nz, join, 0)
        for d in range(1, nx):
            x_send(d).start()

    def weight_z():
        for d in range(1, nx):
            x_send(d).wait_recv()

        def join(k, carry):
            total = wx[px * nz + k].astype(F32)
            for d in range(nx - 1):
                total = total + wxr[d, k].astype(F32)
            wz[k] = total.astype(BF16)
            return carry

        lax.fori_loop(0, nz, join, 0)
        for d in range(1, nz):
            z_send(d).start()

    def weight_end():
        total = wz[pz].astype(F32)
        for d in range(1, nz):
            z_send(d).wait_recv()
            total = total + wzr[d - 1].astype(F32)
        wg_out[...] = total * scale

    def feature_step(i):
        @pl.when(i == 0)
        def _():
            emb_copy.wait()

        @pl.when(section > 0)
        def _():
            p_copy(i * sections).wait_recv()

        p = pbuf[pl.ds(pl.multiple_of(i * rows, rows), rows), :]
        s = dot(p, fold[...], NN).astype(BF16)
        blocks = hidden // 128
        tall = jnp.concatenate([s[:, 128 * b:128 * b + 128] for b in range(blocks)], axis=0)
        per = 128 // features
        own_row = lax.rem(lax.broadcasted_iota(jnp.int32, (rows, wide), 0), GROUP)
        own_lane = lax.broadcasted_iota(jnp.int32, (rows, wide), 1) // features
        for j in range(per):
            e = dot(tall, pick[j], NN)
            for b in range(blocks):
                kept = jnp.where(own_row == own_lane, e[rows * b:rows * b + rows], 0.0)
                spread[b * per + j] = kept.astype(BF16)
        for g in range(rows // GROUP):
            lhs = spread[:, GROUP * g:GROUP * g + GROUP, :].reshape(features * GROUP, wide)
            at = pl.multiple_of((i * (rows // GROUP) + g) * wide, wide)
            out = dot(lhs, emb_v[pl.ds(at, wide), :], NN)
            fg[i, :, GROUP * g:GROUP * g + GROUP, :] = out.astype(BF16).reshape(features, GROUP, lanes)

        core = lax.rem(i, 2)
        slot = pl.ds(pl.multiple_of((pz * 2 + pc) * rows, rows), rows)

        def send(n, carry):
            tx, tz = chip(n)
            src = fg.at[i, tx * nz + tz]
            dst = arr.at[i // 2, px, slot]
            home = (n == 0) & (pc == core)

            @pl.when(home)
            def _():
                pltpu.make_async_copy(src, dst, f_recv.at[i // 2, px]).start()

            @pl.when(jnp.logical_not(home))
            def _():
                remote(src, dst, f_send.at[i], f_recv.at[i // 2, px],
                       {"owner_0": tx, "owner_1": tz, "owner_2": core}).start()
            return carry

        lax.fori_loop(0, nx * nz, send, 0)

    table_rows = acc.shape[0]

    def table_step(i):
        h = i // 2

        @pl.when(h == 0)
        def _():
            pltpu.make_async_copy(idr, idr, id_recv).wait()

        row = lax.broadcasted_iota(jnp.int32, (table_rows, 2 * rows), 0)

        def gather(g, carry):
            pltpu.make_async_copy(arr.at[h, g], arr.at[h, g], f_recv.at[h, g]).wait()
            for z in range(nz):
                both = idr[(g * nz + z) * 2] + idr[(g * nz + z) * 2 + 1]
                ids = jnp.where(h == 0, both[:, :2 * rows], both[:, 2 * rows:])
                onehot[:, z * 2 * rows:(z + 1) * 2 * rows] = jnp.where(row == ids, 1.0, 0.0).astype(BF16)
            acc[...] = acc[...] + dot(onehot[...], arr[h, g], NN)
            return carry

        lax.fori_loop(0, nx, gather, 0)

    first = jnp.where(last, chunks + 1, jnp.where(section == 0, 0, 4 * section + 1))
    ends = chunks + 1 + 4 * micros + 8

    def tick(now, carry):
        @pl.when(now < chunks)
        def _():
            chain_step(now)

        @pl.when((now < chunks) & (lax.rem(now, sections) == sections - 1))
        def _():
            @pl.when(now == sections - 1)
            def _():
                x_copy.wait()
            weight_step(now // sections)

        @pl.when(now == chunks)
        def _():
            core_copy.start()

        @pl.when(now == chunks + 1)
        def _():
            weight_x()

        lag = now - first

        @pl.when((lag >= 0) & (lax.rem(lag, 4) == 0) & (lag < 4 * micros))
        def _():
            feature_step(lag // 4)

        late = lag - 7

        @pl.when((late >= 0) & (lax.rem(late, 4) == 0) & (late < 4 * micros) & (lax.rem(late // 4, 2) == pc))
        def _():
            table_step(late // 4)

        @pl.when(now == chunks + 4)
        def _():
            weight_z()

        @pl.when(now == chunks + 8)
        def _():
            weight_end()
        return carry

    lax.fori_loop(0, ends, tick, 0)

    half = table_rows // 2
    sib_copy = remote(part(acc, 1 - pc, half), sib, sib_send, sib_recv, sibling)
    sib_copy.start()
    sib_copy.wait()
    mine = pl.ds(pl.multiple_of(pc * half, half), half)
    sib[...] = sib[...] + acc[mine, :]
    piece = half // sections

    def y_copy(d):
        to = lax.rem(section + d, sections)
        return remote(part(sib, to, piece), yrecv.at[d - 1], y_send.at[d - 1], y_recv.at[d - 1],
                      {"section": to})

    for d in range(1, sections):
        y_copy(d).start()
    total = part(sib, section, piece)[...]
    for d in range(1, sections):
        y_copy(d).wait_recv()
        total = total + yrecv[d - 1]
    tg_out[...] = total * scale

    def finish(t, carry):
        @pl.when(section > 0)
        def _():
            down_copy(t).wait_send()

        @pl.when((section == 0) & (lax.rem(t, sections) > 0))
        def _():
            p_copy(t).wait_send()
        return carry

    lax.fori_loop(0, chunks, finish, 0)
    some = pl.ds(0, 2 * nx * nz - 1)
    pltpu.make_async_copy(ids_v.at[some], ids_v.at[some], id_send).wait()
    for i in range(micros):
        @pl.when(pc == i % 2)
        def _():
            sent = fg.at[i, pl.ds(0, features - 1)]
            pltpu.make_async_copy(sent, sent, f_send.at[i]).wait()

        @pl.when(pc != i % 2)
        def _():
            sent = fg.at[i]
            pltpu.make_async_copy(sent, sent, f_send.at[i]).wait()
    core_copy.wait_send()
    for d in range(1, nx):
        x_send(d).wait_send()
    for d in range(1, nz):
        z_send(d).wait_send()
    for d in range(1, sections):
        y_copy(d).wait_send()


def per_device(weights, inputs, preact, cotangent, embeddings, row_ids):
    sections = lax.axis_size("section")
    nx, nz, cores = (lax.axis_size(a) for a in OWNER)
    micros, batch_rows, hidden = cotangent.shape
    quarter, features, width = embeddings.shape[1:]
    total = micros * batch_rows
    owners = nx * nz * cores
    scale = 1.0 / math.sqrt(total * owners)
    table_rows = 1024
    ids = jnp.transpose(row_ids, (2, 0, 1)).reshape(features, micros // 2, 2, quarter)
    ids = jnp.transpose(ids, (0, 2, 1, 3))[:, :, :, None, :]
    core = lax.axis_index("owner_2")
    ids = jnp.where(jnp.arange(2).reshape(1, 1, 1, 2, 1) == core, ids, 0)
    ids = ids.reshape(owners, 1, 2 * cores * quarter)
    dma = pltpu.SemaphoreType.DMA
    vmem = pl.BlockSpec(memory_space=pltpu.VMEM)
    hbm = pl.BlockSpec(memory_space=pl.ANY)
    chunks = micros * sections
    rows = total // chunks
    wide = GROUP * features
    part = hidden // owners
    half = table_rows // 2
    V = pltpu.VMEM
    weight_grad, table_grad = pl.pallas_call(
        functools.partial(step_kernel, (micros, sections, nx, nz, features), scale),
        out_shape=(
            jax.ShapeDtypeStruct((part, hidden), F32),
            jax.ShapeDtypeStruct((half // sections, width), F32),
        ),
        in_specs=[hbm] * 6,
        out_specs=(vmem, vmem),
        scratch_shapes=[
            V((hidden, hidden), BF16),
            V((total, hidden), BF16),
            V((total, hidden), BF16),
            V((micros * quarter * features, width), BF16),
            V(ids.shape, jnp.int32),
            V((total, hidden), BF16),
            V((total, hidden), BF16),
            V((total, hidden), BF16),
            V((micros * quarter, hidden), BF16),
            V((nx * nz, 2, part, hidden), F32),
            V((nx * nz, part, hidden), F32),
            V((nx * nz, part, hidden), BF16),
            V((nx - 1, nz, part, hidden), BF16),
            V((nz, part, hidden), BF16),
            V((nz - 1, part, hidden), BF16),
            V((hidden, hidden), BF16),
            V((128 // features, 128, wide), BF16),
            V((features, rows, wide), BF16),
            V((micros, features, rows, width), BF16),
            V((micros // 2, nx, nz * 2 * rows, width), BF16),
            V(ids.shape, jnp.int32),
            V((table_rows, nz * 2 * rows), BF16),
            V((table_rows, width), F32),
            V((half, width), F32),
            V((sections - 1, half // sections, width), F32),
            dma, dma, dma((chunks,)), dma, dma, dma((chunks,)), dma((chunks,)),
            dma((micros,)), dma((chunks,)),
            dma, dma, dma((micros,)), dma((micros // 2, nx)),
            dma, dma, dma((nx - 1,)), dma((nx - 1,)), dma((nz - 1,)), dma((nz - 1,)),
            dma, dma, dma((sections - 1,)), dma((sections - 1,)),
        ],
        compiler_params=pltpu.CompilerParams(
            collective_id=0, has_side_effects=True, vmem_limit_bytes=60 * 1024 * 1024
        ),
    )(
        weights[0],
        inputs.reshape(total, hidden),
        preact.reshape(total, hidden),
        cotangent.reshape(total, hidden),
        embeddings.reshape(micros * quarter * features, width),
        ids,
    )
    return (weight_grad[None], table_grad[None])


def solution(mesh):
    finer = Mesh(
        mesh.devices.reshape(mesh.shape["section"], 4, 8, 2),
        ("section", "owner_0", "owner_1", "owner_2"),
    )
    placed = (
        P("section", None, None),
        P("section", None, OWNER, None),
        P("section", None, OWNER, None),
        P(None, OWNER, None),
        P(None, OWNER_SECTION, None, None),
        P(None, OWNER_SECTION, None),
    )
    return jax.shard_map(
        per_device,
        mesh=finer,
        in_specs=placed,
        out_specs=(P("section", OWNER, None), P(OWNER, "section", None)),
        check_vma=False,
    )
```

time: 231 us -> 124 us (0.54)
  the two profiles are of different devices: /device:TPU:8 before, /device:TPU:1 now
where the time goes in v2:
time: 124 us; the launch traced here: 123 us
  Pallas kernels  118 us (95%)
  local copies, waits for them, and re-layouts  4.19 us (3%)
    pallas_call x1, Pallas kernels, per_device(): pl.pallas_call(functools.partial(step_kernel, (micros, sections, nx, nz,...  118 us
    unnamed x2, local copies, waits for them, and re-layouts  2.95 us

profile of v2, /device:TPU:1, one launch (start us, length us, event | category | flops | bytes accessed | tf_op | source)
XLA Modules:
  0.0 123.1 jit_solution(2949391770467056861)
XLA Ops:
  0.6 0.9 copy.8
  1.6 0.1 broadcast_in_dim.37
  1.7 0.1 broadcast_in_dim.33
  1.8 0.1 broadcast_in_dim.34
  1.9 0.7 broadcast_select_fusion.ids_hbm
  2.6 117.5 %shard_map.77 = (f32[16,1024]{1,0:T(8,128)}, f32[128,128]{1,0:T(8,128)}) custom-call(bf16[1024,1024]{1,0:T(8,128)(2,1)} %bitcast.12, bf16[1024,1024]{1,0:T(8,128)(2,1)} %bitcast.13, bf16[1024,1024]{1,0:T(8,128)(2,1)} %bitcast.14, bf16[1024,1024]{1,0:T(8,128)(2,1)} %bitcast.15, bf16[8192,128]{1,0:T(8,128)(2,1)} %bitcast.16, ...), custom_call_target="tpu_custom_call" | custom-call | tf_op jit(solution)/shard_map/pallas_call | solution.py:458
  120.1 1.5 %copy.11 = f32[1,16,1024]{2,1,0:T(8,128)} copy(f32[1,16,1024]{2,1,0:T(8,128)} %bitcast.19) | data formatting | bytes 131072
  121.6 1.5 %copy.12 = f32[1,128,128]{2,1,0:T(8,128)} copy(f32[1,128,128]{2,1,0:T(8,128)} %bitcast.18) | data formatting | bytes 131072
  (2 shorter events, 0.1 us)

commit v3 on v2

--- a/solution.py
+++ b/solution.py
@@ -28,9 +28,9 @@
     dims, scale,
     w_hbm, x_hbm, pre_hbm, cot_hbm, emb_hbm, ids_hbm,
     wg_out, tg_out,
-    w_v, x_v, pre_v, emb_v, ids_v, rbuf, sbuf, slopes, pbuf, wacc, wrecv, wx, wxr, wz, wzr,
-    fold, pick, spread, fg, arr, idr, onehot, acc, sib, yrecv,
-    w_sem, x_sem, pre_sem, emb_sem, ids_sem, in_sem, out_sem, p_recv, p_send,
+    w_v, wt_v, x_v, pre_v, emb_v, ids_v, rbuf, sbuf, slopes, pbuf, wacc, wsend, wrecv, wx, wxr, wz, wzr,
+    fold, pick, spread, fg, arr, idr, onehot, acc, sib, ysend, yrecv,
+    near, w_sem, x_sem, pre_sem, emb_sem, ids_sem, in_sem, out_sem, p_recv, p_send,
     id_send, id_recv, f_send, f_recv, ac_send, ac_recv, bx_send, bx_recv, cz_send, cz_recv,
     sib_send, sib_recv, y_send, y_recv,
 ):
@@ -39,8 +39,10 @@
     px = lax.axis_index("owner_0")
     pz = lax.axis_index("owner_1")
     pc = lax.axis_index("owner_2")
-    chunks = micros * sections
-    rows = pre_v.shape[0] // chunks
+    rows = pre_v.shape[0] // (micros * sections)
+    fine = rows // 2
+    small = 2 * sections
+    chunks = small + (micros - 1) * sections
     hidden = w_v.shape[0]
     lanes = emb_v.shape[1]
     last = section == sections - 1
@@ -48,11 +50,29 @@
     def part(ref, t, size):
         return ref.at[pl.ds(pl.multiple_of(t * size, size), size)]
 
-    def pre_copy(t):
-        return pltpu.make_async_copy(part(pre_hbm, t, rows), part(pre_v, t, rows), pre_sem.at[t])
-
-    def cot_copy(t):
-        return pltpu.make_async_copy(part(cot_hbm, t, rows), part(rbuf, t, rows), in_sem.at[t])
+    def spot(t, size):
+        start = t * fine if size == fine else small * fine + (t - small) * rows
+        return pl.ds(pl.multiple_of(start, fine), size)
+
+    def each_chunk(body):
+        def narrow(t, carry):
+            body(t, fine)
+            return carry
+
+        def broad(t, carry):
+            body(t, rows)
+            return carry
+
+        lax.fori_loop(0, small, narrow, 0)
+        lax.fori_loop(small, chunks, broad, 0)
+
+    def pre_copy(t, size):
+        at = spot(t, size)
+        return pltpu.make_async_copy(pre_hbm.at[at], pre_v.at[at], pre_sem.at[t])
+
+    def cot_copy(t, size):
+        at = spot(t, size)
+        return pltpu.make_async_copy(cot_hbm.at[at], rbuf.at[at], in_sem.at[t])
 
     def remote(src, dst, send, recv, where):
         return pltpu.make_async_remote_copy(
@@ -60,16 +80,24 @@
             device_id=where, device_id_type=MESH,
         )
 
-    def down_copy(t):
+    def down_copy(t, size):
+        at = spot(t, size)
         return remote(
-            part(sbuf, t, rows), part(rbuf, t, rows), out_sem.at[t], in_sem.at[t],
+            sbuf.at[at], rbuf.at[at], out_sem.at[t], in_sem.at[t],
             {"section": lax.rem(section + sections - 1, sections)},
         )
 
-    def p_copy(t):
+    def p_place(t, size):
+        if size == fine:
+            return t // 2, 0, lax.rem(t, 2) * fine
+        unit = (t - small) // sections + 1
+        return lax.rem(t, sections), unit, unit * rows
+
+    def p_copy(t, size):
+        to, unit, start = p_place(t, size)
         return remote(
-            part(sbuf, t, rows), part(pbuf, t // sections, rows),
-            p_send.at[t], p_recv.at[t // sections], {"section": lax.rem(t, sections)},
+            sbuf.at[spot(t, size)], pbuf.at[pl.ds(pl.multiple_of(start, fine), size)],
+            p_send.at[t], p_recv.at[unit], {"section": to},
         )
 
     def chip(n):
@@ -84,63 +112,57 @@
     ids_copy = pltpu.make_async_copy(ids_hbm, ids_v, ids_sem)
     w_copy.start()
 
-    def begin(t, carry):
-        pre_copy(t).start()
+    def begin(t, size):
+        pre_copy(t, size).start()
 
         @pl.when(last)
         def _():
-            cot_copy(t).start()
-        return carry
-
-    lax.fori_loop(0, chunks, begin, 0)
+            cot_copy(t, size).start()
+
+    each_chunk(begin)
     ids_copy.start()
     emb_copy.start()
     x_copy.start()
 
     barrier = pltpu.get_barrier_semaphore()
-    for d in range(1, sections):
-        pl.semaphore_signal(
-            barrier, inc=1, device_id={"section": lax.rem(section + d, sections)},
-            device_id_type=MESH,
-        )
-
-    def greet(n, carry):
-        tx, tz = chip(n)
-
-        def hail(core):
+
+    def peers(name, place, count, sem):
+        for d in range(1, count):
             pl.semaphore_signal(
-                barrier, inc=1, device_id={"owner_0": tx, "owner_1": tz, "owner_2": core},
-                device_id_type=MESH,
+                sem, inc=1, device_id={name: lax.rem(place + d, count)}, device_id_type=MESH
             )
 
-        hail(1 - pc)
-
-        @pl.when(n > 0)
-        def _():
-            hail(pc)
-        return carry
-
-    lax.fori_loop(0, nx * nz, greet, 0)
-
-    across = lax.broadcasted_iota(jnp.int32, (128, hidden), 1)
-    flipped = lax.rem(across, features) * features + across // features
-
-    def make_fold(b, carry):
-        down = lax.broadcasted_iota(jnp.int32, (128, hidden), 0) + b * 128
-        value = jnp.where(down == across, 1.0, 0.0) + jnp.where(down == flipped, 1.0, 0.0)
-        part(fold, b, 128)[...] = value.astype(BF16)
-        return carry
-
-    lax.fori_loop(0, hidden // 128, make_fold, 0)
+    inner = (("owner_1", pz, nz), ("owner_0", px, nx), ("owner_2", pc, 2))
+    peers("section", section, sections, barrier)
+
+    @pl.when(section == 0)
+    def _():
+        for name, place, count in inner:
+            peers(name, place, count, barrier)
+        pl.semaphore_wait(barrier, sections - 1 + sum(count - 1 for name, place, count in inner))
+
+    @pl.when(section > 0)
+    def _():
+        pl.semaphore_wait(barrier, sections - 1)
+
     wide = GROUP * features
-    for j in range(128 // features):
-        down = lax.broadcasted_iota(jnp.int32, (128, wide), 0)
-        col = lax.rem(lax.broadcasted_iota(jnp.int32, (128, wide), 1), features) + j * features
-        pick[j] = jnp.where(down == col, 1.0, 0.0).astype(BF16)
-    acc[...] = jnp.zeros_like(acc)
-
-    pl.semaphore_wait(barrier, sections - 1 + 2 * nx * nz - 1)
-    ids_copy.wait()
+
+    def prepare():
+        across = lax.broadcasted_iota(jnp.int32, (128, hidden), 1)
+        flipped = lax.rem(across, features) * features + across // features
+
+        def make_fold(b, carry):
+            down = lax.broadcasted_iota(jnp.int32, (128, hidden), 0) + b * 128
+            value = jnp.where(down == across, 1.0, 0.0) + jnp.where(down == flipped, 1.0, 0.0)
+            part(fold, b, 128)[...] = value.astype(BF16)
+            return carry
+
+        lax.fori_loop(0, hidden // 128, make_fold, 0)
+        for j in range(128 // features):
+            down = lax.broadcasted_iota(jnp.int32, (128, wide), 0)
+            col = lax.rem(lax.broadcasted_iota(jnp.int32, (128, wide), 1), features) + j * features
+            pick[j] = jnp.where(down == col, 1.0, 0.0).astype(BF16)
+        acc[...] = jnp.zeros_like(acc)
 
     def send_ids(n, carry):
         tx, tz = chip(n)
@@ -161,38 +183,74 @@
                 ).start()
         return carry
 
-    lax.fori_loop(0, nx * nz, send_ids, 0)
+    @pl.when(section == 0)
+    def _():
+        peers(*inner[0], near.at[0])
+
+    def meet(stage):
+        pl.semaphore_wait(near.at[stage], inner[stage][2] - 1)
+        if stage < 2:
+            peers(*inner[stage + 1], near.at[stage + 1])
+        else:
+            peers("section", section, sections, near.at[3])
+
+    def exchange_ids():
+        @pl.when(section > 0)
+        def _():
+            pl.semaphore_wait(near.at[3], 1)
+
+        ids_copy.wait()
+        lax.fori_loop(0, nx * nz, send_ids, 0)
+
     w_copy.wait()
 
-    def chain_step(t):
-        pre_copy(t).wait()
+    @pl.when(jnp.logical_not(last))
+    def _():
+        def turn(b, carry):
+            cols = pl.ds(pl.multiple_of(b * 128, 128), 128)
+            wt_v[:, cols] = part(w_v, b, 128)[...].T
+            return carry
+
+        lax.fori_loop(0, hidden // 128, turn, 0)
+        prepare()
+
+    def chain_step(t, size):
+        pre_copy(t, size).wait()
 
         @pl.when(last)
         def _():
-            cot_copy(t).wait()
+            cot_copy(t, size).wait()
 
         @pl.when(jnp.logical_not(last))
         def _():
-            down_copy(t).wait_recv()
-
-        at = pl.ds(pl.multiple_of(t * rows, rows), rows)
+            down_copy(t, size).wait_recv()
+
+        at = spot(t, size)
         incoming = rbuf[at, :]
         slope = jnp.where(pre_v[at, :] > 0, incoming, jnp.zeros_like(incoming))
         slopes[at, :] = slope
-        sbuf[at, :] = dot(slope, w_v[...], NT).astype(BF16)
+
+        @pl.when(last)
+        def _():
+            sbuf[at, :] = dot(slope, w_v[...], NT).astype(BF16)
+
+        @pl.when(jnp.logical_not(last))
+        def _():
+            sbuf[at, :] = dot(slope, wt_v[...], NN).astype(BF16)
 
         @pl.when(section > 0)
         def _():
-            down_copy(t).start()
-
-        @pl.when((section == 0) & (lax.rem(t, sections) > 0))
-        def _():
-            p_copy(t).start()
-
-        @pl.when((section == 0) & (lax.rem(t, sections) == 0))
-        def _():
-            own = pl.multiple_of((t // sections) * rows, rows)
-            pbuf[pl.ds(own, rows), :] = sbuf[at, :]
+            down_copy(t, size).start()
+
+        to, unit, start = p_place(t, size)
+
+        @pl.when((section == 0) & (to > 0))
+        def _():
+            p_copy(t, size).start()
+
+        @pl.when((section == 0) & (to == 0))
+        def _():
+            pbuf[pl.ds(pl.multiple_of(start, fine), size), :] = sbuf[at, :]
 
     block = 256
 
@@ -218,7 +276,15 @@
         lax.fori_loop(0, hidden // block, column, 0)
 
     sibling = {"owner_2": 1 - pc}
-    core_copy = remote(wacc.at[:, 1 - pc], wrecv, ac_send, ac_recv, sibling)
+    core_copy = remote(wsend, wrecv, ac_send, ac_recv, sibling)
+
+    def weight_core():
+        def cast(k, carry):
+            wsend[k] = wacc[k, 1 - pc].astype(BF16)
+            return carry
+
+        lax.fori_loop(0, nx * nz, cast, 0)
+        core_copy.start()
 
     def x_send(d):
         to = lax.rem(px + d, nx)
@@ -234,7 +300,7 @@
         core_copy.wait_recv()
 
         def join(k, carry):
-            wx[k] = (wacc[k, pc] + wrecv[k]).astype(BF16)
+            wx[k] = (wacc[k, pc] + wrecv[k].astype(F32)).astype(BF16)
             return carry
 
         lax.fori_loop(0, nx * nz, join, 0)
@@ -270,7 +336,8 @@
 
         @pl.when(section > 0)
         def _():
-            p_copy(i * sections).wait_recv()
+            here = part(pbuf, i, rows)
+            pltpu.make_async_copy(here, here, p_recv.at[i]).wait()
 
         p = pbuf[pl.ds(pl.multiple_of(i * rows, rows), rows), :]
         s = dot(p, fold[...], NN).astype(BF16)
@@ -333,48 +400,83 @@
 
         lax.fori_loop(0, nx, gather, 0)
 
-    first = jnp.where(last, chunks + 1, jnp.where(section == 0, 0, 4 * section + 1))
-    ends = chunks + 1 + 4 * micros + 8
+    def by_section(*values):
+        chosen = values[-1]
+        for n in range(sections - 1):
+            chosen = jnp.where(section == n, values[n], chosen)
+        return chosen
+
+    features_at = (
+        by_section(7, 9, 12, 21), by_section(9, 13, 16, 26),
+        by_section(12, 17, 20, 30), by_section(16, 20, 22, 34),
+    )
+    tables_at = (
+        by_section(14, 21, 21, 31), by_section(21, 21, 23, 35),
+        by_section(21, 22, 24, 36), by_section(22, 24, 25, 37),
+    )
+    meet_time = by_section(7, 9, 12, 19)
+    x_time = by_section(20, 21, 21, 22)
+    z_time = by_section(23, 23, 23, 27)
+    ends = 38
 
     def tick(now, carry):
-        @pl.when(now < chunks)
-        def _():
-            chain_step(now)
-
-        @pl.when((now < chunks) & (lax.rem(now, sections) == sections - 1))
-        def _():
-            @pl.when(now == sections - 1)
+        for stage in range(3):
+            @pl.when((section == 0) & (now == stage))
+            def _():
+                meet(stage)
+
+        @pl.when(now < small)
+        def _():
+            chain_step(now, fine)
+
+        @pl.when((now >= small) & (now < chunks))
+        def _():
+            chain_step(now, rows)
+
+        @pl.when(now == meet_time)
+        def _():
+            exchange_ids()
+
+        @pl.when(last & (now == 6))
+        def _():
+            prepare()
+
+        done = now + 1 - small
+
+        @pl.when((now < chunks) & (done >= 0) & (lax.rem(done, sections) == 0))
+        def _():
+            @pl.when(done == 0)
             def _():
                 x_copy.wait()
-            weight_step(now // sections)
+            weight_step(done // sections)
 
         @pl.when(now == chunks)
         def _():
-            core_copy.start()
-
-        @pl.when(now == chunks + 1)
+            weight_core()
+
+        which = micros
+        for n in range(micros):
+            which = jnp.where(now == features_at[n], n, which)
+
+        @pl.when(which < micros)
+        def _():
+            feature_step(which)
+
+        @pl.when(now == x_time)
         def _():
             weight_x()
 
-        lag = now - first
-
-        @pl.when((lag >= 0) & (lax.rem(lag, 4) == 0) & (lag < 4 * micros))
-        def _():
-            feature_step(lag // 4)
-
-        late = lag - 7
-
-        @pl.when((late >= 0) & (lax.rem(late, 4) == 0) & (late < 4 * micros) & (lax.rem(late // 4, 2) == pc))
-        def _():
-            table_step(late // 4)
-
-        @pl.when(now == chunks + 4)
+        @pl.when(now == z_time)
         def _():
             weight_z()
 
-        @pl.when(now == chunks + 8)
-        def _():
-            weight_end()
+        unit = micros
+        for n in range(micros):
+            unit = jnp.where((now == tables_at[n]) & (pc == n % 2), n, unit)
+
+        @pl.when(unit < micros)
+        def _():
+            table_step(unit)
         return carry
 
     lax.fori_loop(0, ends, tick, 0)
@@ -385,32 +487,33 @@
     sib_copy.wait()
     mine = pl.ds(pl.multiple_of(pc * half, half), half)
     sib[...] = sib[...] + acc[mine, :]
+    ysend[...] = sib[...].astype(BF16)
     piece = half // sections
 
     def y_copy(d):
         to = lax.rem(section + d, sections)
-        return remote(part(sib, to, piece), yrecv.at[d - 1], y_send.at[d - 1], y_recv.at[d - 1],
+        return remote(part(ysend, to, piece), yrecv.at[d - 1], y_send.at[d - 1], y_recv.at[d - 1],
                       {"section": to})
 
     for d in range(1, sections):
         y_copy(d).start()
+    weight_end()
     total = part(sib, section, piece)[...]
     for d in range(1, sections):
         y_copy(d).wait_recv()
-        total = total + yrecv[d - 1]
+        total = total + yrecv[d - 1].astype(F32)
     tg_out[...] = total * scale
 
-    def finish(t, carry):
+    def finish(t, size):
         @pl.when(section > 0)
         def _():
-            down_copy(t).wait_send()
-
-        @pl.when((section == 0) & (lax.rem(t, sections) > 0))
-        def _():
-            p_copy(t).wait_send()
-        return carry
-
-    lax.fori_loop(0, chunks, finish, 0)
+            down_copy(t, size).wait_send()
+
+        @pl.when((section == 0) & (p_place(t, size)[0] > 0))
+        def _():
+            p_copy(t, size).wait_send()
+
+    each_chunk(finish)
     some = pl.ds(0, 2 * nx * nz - 1)
     pltpu.make_async_copy(ids_v.at[some], ids_v.at[some], id_send).wait()
     for i in range(micros):
@@ -449,8 +552,8 @@
     dma = pltpu.SemaphoreType.DMA
     vmem = pl.BlockSpec(memory_space=pltpu.VMEM)
     hbm = pl.BlockSpec(memory_space=pl.ANY)
-    chunks = micros * sections
-    rows = total // chunks
+    chunks = (micros + 1) * sections
+    rows = total // (micros * sections)
     wide = GROUP * features
     part = hidden // owners
     half = table_rows // 2
@@ -465,6 +568,7 @@
         out_specs=(vmem, vmem),
         scratch_shapes=[
             V((hidden, hidden), BF16),
+            V((hidden, hidden), BF16),
             V((total, hidden), BF16),
             V((total, hidden), BF16),
             V((micros * quarter * features, width), BF16),
@@ -474,7 +578,8 @@
             V((total, hidden), BF16),
             V((micros * quarter, hidden), BF16),
             V((nx * nz, 2, part, hidden), F32),
-            V((nx * nz, part, hidden), F32),
+            V((nx * nz, part, hidden), BF16),
+            V((nx * nz, part, hidden), BF16),
             V((nx * nz, part, hidden), BF16),
             V((nx - 1, nz, part, hidden), BF16),
             V((nz, part, hidden), BF16),
@@ -488,7 +593,9 @@
             V((table_rows, nz * 2 * rows), BF16),
             V((table_rows, width), F32),
             V((half, width), F32),
-            V((sections - 1, half // sections, width), F32),
+            V((half, width), BF16),
+            V((sections - 1, half // sections, width), BF16),
+            pltpu.SemaphoreType.REGULAR((4,)),
             dma, dma, dma((chunks,)), dma, dma, dma((chunks,)), dma((chunks,)),
             dma((micros,)), dma((chunks,)),
             dma, dma, dma((micros,)), dma((micros // 2, nx)),

time: 124 us -> 108 us (0.87)
  Pallas kernels: 118 us -> 102 us
    pallas_call x1, Pallas kernels: 118 us -> 102 us  [per_device(): pl.pallas_call(functools.partial(step_kernel, (micros, sections, nx, nz,...]
where the time goes in v3:
time: 108 us
  Pallas kernels  102 us (94%)
  local copies, waits for them, and re-layouts  4.19 us (4%)
    pallas_call x1, Pallas kernels, per_device(): pl.pallas_call(functools.partial(step_kernel, (micros, sections, nx, nz,...  102 us
    unnamed x2, local copies, waits for them, and re-layouts  2.95 us

profile of v3, /device:TPU:1, one launch (start us, length us, event | category | flops | bytes accessed | tf_op | source)
XLA Modules:
  0.0 107.9 jit_solution(10707150733855795846)
XLA Ops:
  0.6 0.9 copy.8
  1.6 0.1 broadcast_in_dim.37
  1.7 0.1 broadcast_in_dim.33
  1.8 0.1 broadcast_in_dim.34
  1.9 0.7 broadcast_select_fusion.ids_hbm
  2.6 102.3 %shard_map.77 = (f32[16,1024]{1,0:T(8,128)}, f32[128,128]{1,0:T(8,128)}) custom-call(bf16[1024,1024]{1,0:T(8,128)(2,1)} %bitcast.12, bf16[1024,1024]{1,0:T(8,128)(2,1)} %bitcast.13, bf16[1024,1024]{1,0:T(8,128)(2,1)} %bitcast.14, bf16[1024,1024]{1,0:T(8,128)(2,1)} %bitcast.15, bf16[8192,128]{1,0:T(8,128)(2,1)} %bitcast.16, ...), custom_call_target="tpu_custom_call" | custom-call | tf_op jit(solution)/shard_map/pallas_call | solution.py:561
  104.9 1.5 %copy.11 = f32[1,16,1024]{2,1,0:T(8,128)} copy(f32[1,16,1024]{2,1,0:T(8,128)} %bitcast.19) | data formatting | bytes 131072
  106.4 1.5 %copy.12 = f32[1,128,128]{2,1,0:T(8,128)} copy(f32[1,128,128]{2,1,0:T(8,128)} %bitcast.18) | data formatting | bytes 131072
  (2 shorter events, 0.1 us)

commit v4 on v3

--- a/solution.py
+++ b/solution.py
@@ -28,11 +28,11 @@
     dims, scale,
     w_hbm, x_hbm, pre_hbm, cot_hbm, emb_hbm, ids_hbm,
     wg_out, tg_out,
-    w_v, wt_v, x_v, pre_v, emb_v, ids_v, rbuf, sbuf, slopes, pbuf, wacc, wsend, wrecv, wx, wxr, wz, wzr,
-    fold, pick, spread, fg, arr, idr, onehot, acc, sib, ysend, yrecv,
+    w_v, wt_v, x_v, pre_v, emb_v, raw_v, ids_v, rbuf, sbuf, slopes, pbuf, wacc, wsend, wrecv, wx, wxr, wz, wzr, vz, vzr, vx, vxr,
+    fold, pick, spread, fg, arr, idr, onehot, acc, sib, ysend, yrecv, fsend, frecv,
     near, w_sem, x_sem, pre_sem, emb_sem, ids_sem, in_sem, out_sem, p_recv, p_send,
-    id_send, id_recv, f_send, f_recv, ac_send, ac_recv, bx_send, bx_recv, cz_send, cz_recv,
-    sib_send, sib_recv, y_send, y_recv,
+    id_send, id_recv, f_send, f_recv, ac_send, ac_recv, bx_send, bx_recv, cz_send, cz_recv, bz_send, bz_recv, cx_send, cx_recv,
+    sib_send, sib_recv, y_send, y_recv, far_send, far_recv,
 ):
     micros, sections, nx, nz, features = dims
     section = lax.axis_index("section")
@@ -109,7 +109,7 @@
     w_copy = pltpu.make_async_copy(w_hbm, w_v, w_sem)
     x_copy = pltpu.make_async_copy(x_hbm, x_v, x_sem)
     emb_copy = pltpu.make_async_copy(emb_hbm, emb_v, emb_sem)
-    ids_copy = pltpu.make_async_copy(ids_hbm, ids_v, ids_sem)
+    ids_copy = pltpu.make_async_copy(ids_hbm, raw_v, ids_sem)
     w_copy.start()
 
     def begin(t, size):
@@ -163,13 +163,30 @@
             col = lax.rem(lax.broadcasted_iota(jnp.int32, (128, wide), 1), features) + j * features
             pick[j] = jnp.where(down == col, 1.0, 0.0).astype(BF16)
         acc[...] = jnp.zeros_like(acc)
+        ids_copy.wait()
+        owner_lane = lax.rem(lax.broadcasted_iota(jnp.int32, (features, 4 * rows), 1) // rows, 2)
+        for r in range(2):
+            first, second = raw_v[r], raw_v[2 + r]
+            spaced = jnp.concatenate([first, first, second, second], axis=1)
+            spaced = jnp.where(owner_lane == pc, spaced, 0)
+            for f in range(features):
+                ids_v[f * 2 + r] = spaced[f:f + 1, :]
+
+    near_z = nz // 2 + 1
+
+    def gather_at(n):
+        tx, tz = chip(n)
+        k = n // nx
+        far = k >= near_z
+        home = (lax.rem(n, nx) == 0) & ((k == 0) | (k == nz - 1))
+        return tx, lax.rem(tz + jnp.where(far, nz // 2, 0), nz), k, home, tx * nz + tz
 
     def send_ids(n, carry):
-        tx, tz = chip(n)
-        mine = (px * nz + pz) * 2 + pc
+        tx, cz, k, own_chip, feature = gather_at(n)
+        mine = (px * nz + k) * 2 + pc
         for r in range(2):
-            there = (tx * nz + tz) * 2 + r
-            home = (n == 0) & (pc == r)
+            there = feature * 2 + r
+            home = own_chip & (pc == r)
 
             @pl.when(home)
             def _():
@@ -179,7 +196,7 @@
             def _():
                 remote(
                     ids_v.at[there], idr.at[mine], id_send, id_recv,
-                    {"owner_0": tx, "owner_1": tz, "owner_2": r},
+                    {"owner_0": tx, "owner_1": cz, "owner_2": r},
                 ).start()
         return carry
 
@@ -199,7 +216,6 @@
         def _():
             pl.semaphore_wait(near.at[3], 1)
 
-        ids_copy.wait()
         lax.fori_loop(0, nx * nz, send_ids, 0)
 
     w_copy.wait()
@@ -296,14 +312,30 @@
         return remote(wz.at[to], wzr.at[d - 1], cz_send.at[d - 1], cz_recv.at[d - 1],
                       {"owner_1": to})
 
+    def z_first(d):
+        to = lax.rem(pz + d, nz)
+        return remote(part(vz, to, nx), vzr.at[d - 1], bz_send.at[d - 1], bz_recv.at[d - 1],
+                      {"owner_1": to})
+
+    def x_second(d):
+        to = lax.rem(px + d, nx)
+        return remote(vx.at[to], vxr.at[d - 1], cx_send.at[d - 1], cx_recv.at[d - 1],
+                      {"owner_0": to})
+
+    cut = wx.shape[-1]
+
     def weight_x():
         core_copy.wait_recv()
 
         def join(k, carry):
-            wx[k] = (wacc[k, pc] + wrecv[k].astype(F32)).astype(BF16)
+            both = (wacc[k, pc] + wrecv[k].astype(F32)).astype(BF16)
+            wx[k] = both[:, :cut]
+            vz[lax.rem(k, nz) * nx + k // nz] = both[:, cut:]
             return carry
 
         lax.fori_loop(0, nx * nz, join, 0)
+        for d in range(1, nz):
+            z_first(d).start()
         for d in range(1, nx):
             x_send(d).start()
 
@@ -321,15 +353,33 @@
         lax.fori_loop(0, nz, join, 0)
         for d in range(1, nz):
             z_send(d).start()
+        for d in range(1, nz):
+            z_first(d).wait_recv()
+
+        def join_second(k, carry):
+            total = vz[pz * nx + k].astype(F32)
+            for d in range(nz - 1):
+                total = total + vzr[d, k].astype(F32)
+            vx[k] = total.astype(BF16)
+            return carry
+
+        lax.fori_loop(0, nx, join_second, 0)
+        for d in range(1, nx):
+            x_second(d).start()
 
     def weight_end():
         total = wz[pz].astype(F32)
         for d in range(1, nz):
             z_send(d).wait_recv()
             total = total + wzr[d - 1].astype(F32)
-        wg_out[...] = total * scale
-
-    def feature_step(i):
+        wg_out[:, :cut] = total * scale
+        total = vx[px].astype(F32)
+        for d in range(1, nx):
+            x_second(d).wait_recv()
+            total = total + vxr[d - 1].astype(F32)
+        wg_out[:, cut:] = total * scale
+
+    def feature_open(i):
         @pl.when(i == 0)
         def _():
             emb_copy.wait()
@@ -351,6 +401,8 @@
             for b in range(blocks):
                 kept = jnp.where(own_row == own_lane, e[rows * b:rows * b + rows], 0.0)
                 spread[b * per + j] = kept.astype(BF16)
+
+    def feature_close(i):
         for g in range(rows // GROUP):
             lhs = spread[:, GROUP * g:GROUP * g + GROUP, :].reshape(features * GROUP, wide)
             at = pl.multiple_of((i * (rows // GROUP) + g) * wide, wide)
@@ -358,44 +410,42 @@
             fg[i, :, GROUP * g:GROUP * g + GROUP, :] = out.astype(BF16).reshape(features, GROUP, lanes)
 
         core = lax.rem(i, 2)
-        slot = pl.ds(pl.multiple_of((pz * 2 + pc) * rows, rows), rows)
-
-        def send(n, carry):
-            tx, tz = chip(n)
-            src = fg.at[i, tx * nz + tz]
+        def send(step, carry):
+            tx, cz, k, own_chip, feature = gather_at(nx * nz - 1 - step)
+            arrived = f_recv.at[i // 2, px, jnp.where(k >= near_z, 1, 0)]
+            src = fg.at[i, feature]
+            slot = pl.ds(pl.multiple_of((k * 2 + pc) * rows, rows), rows)
             dst = arr.at[i // 2, px, slot]
-            home = (n == 0) & (pc == core)
+            home = own_chip & (pc == core)
 
             @pl.when(home)
             def _():
-                pltpu.make_async_copy(src, dst, f_recv.at[i // 2, px]).start()
+                pltpu.make_async_copy(src, dst, arrived).start()
 
             @pl.when(jnp.logical_not(home))
             def _():
-                remote(src, dst, f_send.at[i], f_recv.at[i // 2, px],
-                       {"owner_0": tx, "owner_1": tz, "owner_2": core}).start()
+                remote(src, dst, f_send.at[i], arrived,
+                       {"owner_0": tx, "owner_1": cz, "owner_2": core}).start()
             return carry
 
         lax.fori_loop(0, nx * nz, send, 0)
 
-    table_rows = acc.shape[0]
-
-    def table_step(i):
+    table_rows = acc.shape[1]
+
+    def table_part(i, role):
         h = i // 2
-
-        @pl.when(h == 0)
-        def _():
-            pltpu.make_async_copy(idr, idr, id_recv).wait()
-
         row = lax.broadcasted_iota(jnp.int32, (table_rows, 2 * rows), 0)
+        low, high = ((0, near_z), (near_z, nz))[role]
+        span = pl.ds(low * 2 * rows, (high - low) * 2 * rows)
 
         def gather(g, carry):
-            pltpu.make_async_copy(arr.at[h, g], arr.at[h, g], f_recv.at[h, g]).wait()
-            for z in range(nz):
+            landed = arr.at[h, g, span]
+            pltpu.make_async_copy(landed, landed, f_recv.at[h, g, role]).wait()
+            for z in range(low, high):
                 both = idr[(g * nz + z) * 2] + idr[(g * nz + z) * 2 + 1]
                 ids = jnp.where(h == 0, both[:, :2 * rows], both[:, 2 * rows:])
                 onehot[:, z * 2 * rows:(z + 1) * 2 * rows] = jnp.where(row == ids, 1.0, 0.0).astype(BF16)
-            acc[...] = acc[...] + dot(onehot[...], arr[h, g], NN)
+            acc[role] = acc[role] + dot(onehot[:, span], arr[h, g, span, :], NN)
             return carry
 
         lax.fori_loop(0, nx, gather, 0)
@@ -407,17 +457,17 @@
         return chosen
 
     features_at = (
-        by_section(7, 9, 12, 21), by_section(9, 13, 16, 26),
-        by_section(12, 17, 20, 30), by_section(16, 20, 22, 34),
+        (by_section(8, 9, 12, 21), by_section(9, 10, 13, 21)),
+        (by_section(10, 13, 16, 26), by_section(12, 14, 17, 26)),
+        (by_section(13, 17, 21, 30), by_section(14, 18, 21, 30)),
+        (by_section(17, 21, 23, 34), by_section(18, 21, 23, 34)),
     )
-    tables_at = (
-        by_section(14, 21, 21, 31), by_section(21, 21, 23, 35),
-        by_section(21, 22, 24, 36), by_section(22, 24, 25, 37),
-    )
-    meet_time = by_section(7, 9, 12, 19)
-    x_time = by_section(20, 21, 21, 22)
-    z_time = by_section(23, 23, 23, 27)
-    ends = 38
+    far_table = jnp.where(pc == 0, by_section(15, 22, 22, 31), by_section(21, 22, 22, 35))
+    own_table = far_table + by_section(1, 0, 0, 0)
+    meet_time = by_section(5, 8, 10, 19)
+    x_time = by_section(20, 20, 20, 22)
+    z_time = by_section(40, 40, 40, 27)
+    ends = 36
 
     def tick(now, carry):
         for stage in range(3):
@@ -454,13 +504,28 @@
         def _():
             weight_core()
 
-        which = micros
+        opened = micros
+        closed = micros
         for n in range(micros):
-            which = jnp.where(now == features_at[n], n, which)
-
-        @pl.when(which < micros)
-        def _():
-            feature_step(which)
+            opened = jnp.where(now == features_at[n][0], n, opened)
+            closed = jnp.where(now == features_at[n][1], n, closed)
+
+        @pl.when(opened < micros)
+        def _():
+            feature_open(opened)
+
+        @pl.when(closed < micros)
+        def _():
+            feature_close(closed)
+
+        @pl.when(now == far_table)
+        def _():
+            pltpu.make_async_copy(idr, idr, id_recv).wait()
+            table_part(pc, 1)
+
+        @pl.when(now == own_table)
+        def _():
+            table_part(pc, 0)
 
         @pl.when(now == x_time)
         def _():
@@ -469,40 +534,55 @@
         @pl.when(now == z_time)
         def _():
             weight_z()
-
-        unit = micros
-        for n in range(micros):
-            unit = jnp.where((now == tables_at[n]) & (pc == n % 2), n, unit)
-
-        @pl.when(unit < micros)
-        def _():
-            table_step(unit)
         return carry
 
     lax.fori_loop(0, ends, tick, 0)
 
     half = table_rows // 2
-    sib_copy = remote(part(acc, 1 - pc, half), sib, sib_send, sib_recv, sibling)
-    sib_copy.start()
-    sib_copy.wait()
-    mine = pl.ds(pl.multiple_of(pc * half, half), half)
-    sib[...] = sib[...] + acc[mine, :]
-    ysend[...] = sib[...].astype(BF16)
     piece = half // sections
 
-    def y_copy(d):
+    def sib_copy(q):
+        return remote(part(acc.at[q], 1 - pc, half), sib.at[q], sib_send.at[q], sib_recv.at[q], sibling)
+
+    def y_copy(d, q):
         to = lax.rem(section + d, sections)
-        return remote(part(ysend, to, piece), yrecv.at[d - 1], y_send.at[d - 1], y_recv.at[d - 1],
-                      {"section": to})
-
-    for d in range(1, sections):
-        y_copy(d).start()
+        return remote(part(ysend.at[q], to, piece), yrecv.at[d - 1, q],
+                      y_send.at[d - 1, q], y_recv.at[d - 1, q], {"section": to})
+
+    def settle(q):
+        sib_copy(q).wait()
+        mine = pl.ds(pl.multiple_of(pc * half, half), half)
+        sib[q] = sib[q] + acc[q, mine, :]
+        ysend[q] = sib[q].astype(BF16)
+        for d in range(1, sections):
+            y_copy(d, q).start()
+
+    table_part(2 + pc, 1)
+    sib_copy(1).start()
+    table_part(2 + pc, 0)
+    sib_copy(0).start()
+
+    @pl.when(z_time > ends)
+    def _():
+        weight_z()
+
+    settle(1)
+    settle(0)
+
+    def gathered(q):
+        total = part(sib.at[q], section, piece)[...]
+        for d in range(1, sections):
+            y_copy(d, q).wait_recv()
+            total = total + yrecv[d - 1, q].astype(F32)
+        return total
+
+    far_copy = remote(fsend, frecv, far_send, far_recv, {"owner_1": lax.rem(pz + nz // 2, nz)})
+    fsend[...] = gathered(1).astype(BF16)
+    far_copy.start()
+    total = gathered(0)
     weight_end()
-    total = part(sib, section, piece)[...]
-    for d in range(1, sections):
-        y_copy(d).wait_recv()
-        total = total + yrecv[d - 1].astype(F32)
-    tg_out[...] = total * scale
+    far_copy.wait_recv()
+    tg_out[...] = (total + frecv[...].astype(F32)) * scale
 
     def finish(t, size):
         @pl.when(section > 0)
@@ -514,12 +594,12 @@
             p_copy(t, size).wait_send()
 
     each_chunk(finish)
-    some = pl.ds(0, 2 * nx * nz - 1)
+    some = pl.ds(0, 2 * nx * nz - 2)
     pltpu.make_async_copy(ids_v.at[some], ids_v.at[some], id_send).wait()
     for i in range(micros):
         @pl.when(pc == i % 2)
         def _():
-            sent = fg.at[i, pl.ds(0, features - 1)]
+            sent = fg.at[i, pl.ds(0, features - 2)]
             pltpu.make_async_copy(sent, sent, f_send.at[i]).wait()
 
         @pl.when(pc != i % 2)
@@ -529,10 +609,19 @@
     core_copy.wait_send()
     for d in range(1, nx):
         x_send(d).wait_send()
+        x_second(d).wait_send()
     for d in range(1, nz):
         z_send(d).wait_send()
-    for d in range(1, sections):
-        y_copy(d).wait_send()
+        z_first(d).wait_send()
+    for q in range(2):
+        for d in range(1, sections):
+            y_copy(d, q).wait_send()
+    far_copy.wait_send()
+
+
+def hand_on(a_ref, b_ref, a_out, b_out):
+    a_out[...] = a_ref[...]
+    b_out[...] = b_ref[...]
 
 
 def per_device(weights, inputs, preact, cotangent, embeddings, row_ids):
@@ -544,11 +633,7 @@
     owners = nx * nz * cores
     scale = 1.0 / math.sqrt(total * owners)
     table_rows = 1024
-    ids = jnp.transpose(row_ids, (2, 0, 1)).reshape(features, micros // 2, 2, quarter)
-    ids = jnp.transpose(ids, (0, 2, 1, 3))[:, :, :, None, :]
-    core = lax.axis_index("owner_2")
-    ids = jnp.where(jnp.arange(2).reshape(1, 1, 1, 2, 1) == core, ids, 0)
-    ids = ids.reshape(owners, 1, 2 * cores * quarter)
+    ids_shape = (owners, 1, 2 * cores * quarter)
     dma = pltpu.SemaphoreType.DMA
     vmem = pl.BlockSpec(memory_space=pltpu.VMEM)
     hbm = pl.BlockSpec(memory_space=pl.ANY)
@@ -557,6 +642,7 @@
     wide = GROUP * features
     part = hidden // owners
     half = table_rows // 2
+    cut = hidden * 3 // 4
     V = pltpu.VMEM
     weight_grad, table_grad = pl.pallas_call(
         functools.partial(step_kernel, (micros, sections, nx, nz, features), scale),
@@ -572,7 +658,8 @@
             V((total, hidden), BF16),
             V((total, hidden), BF16),
             V((micros * quarter * features, width), BF16),
-            V(ids.shape, jnp.int32),
+            V((micros, features, quarter), jnp.int32),
+            V(ids_shape, jnp.int32),
             V((total, hidden), BF16),
             V((total, hidden), BF16),
             V((total, hidden), BF16),
@@ -580,27 +667,34 @@
             V((nx * nz, 2, part, hidden), F32),
             V((nx * nz, part, hidden), BF16),
             V((nx * nz, part, hidden), BF16),
-            V((nx * nz, part, hidden), BF16),
-            V((nx - 1, nz, part, hidden), BF16),
-            V((nz, part, hidden), BF16),
-            V((nz - 1, part, hidden), BF16),
+            V((nx * nz, part, cut), BF16),
+            V((nx - 1, nz, part, cut), BF16),
+            V((nz, part, cut), BF16),
+            V((nz - 1, part, cut), BF16),
+            V((nx * nz, part, hidden - cut), BF16),
+            V((nz - 1, nx, part, hidden - cut), BF16),
+            V((nx, part, hidden - cut), BF16),
+            V((nx - 1, part, hidden - cut), BF16),
             V((hidden, hidden), BF16),
             V((128 // features, 128, wide), BF16),
             V((features, rows, wide), BF16),
             V((micros, features, rows, width), BF16),
             V((micros // 2, nx, nz * 2 * rows, width), BF16),
-            V(ids.shape, jnp.int32),
+            V(ids_shape, jnp.int32),
             V((table_rows, nz * 2 * rows), BF16),
-            V((table_rows, width), F32),
-            V((half, width), F32),
-            V((half, width), BF16),
-            V((sections - 1, half // sections, width), BF16),
+            V((2, table_rows, width), F32),
+            V((2, half, width), F32),
+            V((2, half, width), BF16),
+            V((sections - 1, 2, half // sections, width), BF16),
+            V((half // sections, width), BF16),
+            V((half // sections, width), BF16),
             pltpu.SemaphoreType.REGULAR((4,)),
             dma, dma, dma((chunks,)), dma, dma, dma((chunks,)), dma((chunks,)),
             dma((micros,)), dma((chunks,)),
-            dma, dma, dma((micros,)), dma((micros // 2, nx)),
+            dma, dma, dma((micros,)), dma((micros // 2, nx, 2)),
             dma, dma, dma((nx - 1,)), dma((nx - 1,)), dma((nz - 1,)), dma((nz - 1,)),
-            dma, dma, dma((sections - 1,)), dma((sections - 1,)),
+            dma((nz - 1,)), dma((nz - 1,)), dma((nx - 1,)), dma((nx - 1,)),
+            dma((2,)), dma((2,)), dma((sections - 1, 2)), dma((sections - 1, 2)), dma, dma,
         ],
         compiler_params=pltpu.CompilerParams(
             collective_id=0, has_side_effects=True, vmem_limit_bytes=60 * 1024 * 1024
@@ -611,8 +705,17 @@
         preact.reshape(total, hidden),
         cotangent.reshape(total, hidden),
         embeddings.reshape(micros * quarter * features, width),
-        ids,
+        row_ids.transpose(0, 2, 1),
     )
+    weight_grad, table_grad = pl.pallas_call(
+        hand_on,
+        out_shape=(
+            jax.ShapeDtypeStruct(weight_grad.shape, F32),
+            jax.ShapeDtypeStruct(table_grad.shape, F32),
+        ),
+        in_specs=[vmem] * 2,
+        out_specs=(vmem, vmem),
+    )(weight_grad, table_grad)
     return (weight_grad[None], table_grad[None])
 
 

time: 108 us -> 101 us (0.935)
  local copies, waits for them, and re-layouts: 4.19 us -> 0 us
  Pallas kernels: 102 us -> 99.9 us
    pallas_call x1, Pallas kernels: 102 us -> 98.4 us  [per_device(): pl.pallas_call(functools.partial(step_kernel, (micros, sections, nx, nz,...]
    unnamed x2 -> x0, local copies, waits for them, and re-layouts: 2.95 us -> none
    pallas_call x0 -> x1, Pallas kernels: none -> 1.53 us  [per_device(): pl.pallas_call(hand_on, out_shape=(jax.ShapeDtypeStruct(weight_grad.shape...]
where the time goes in v4:
time: 101 us
  Pallas kernels  99.9 us (99%)
    pallas_call x1, Pallas kernels, per_device(): pl.pallas_call(functools.partial(step_kernel, (micros, sections, nx, nz,...  98.4 us

profile of v4, /device:TPU:1, one launch (start us, length us, event | category | flops | bytes accessed | tf_op | source)
XLA Modules:
  0.0 100.5 jit_solution(18089443801840505433)
XLA Ops:
  0.6 98.4 %shard_map.77 = (f32[16,1024]{1,0:T(8,128)}, f32[128,128]{1,0:T(8,128)}) custom-call(bf16[1024,1024]{1,0:T(8,128)(2,1)} %bitcast.8, bf16[1024,1024]{1,0:T(8,128)(2,1)} %bitcast.9, bf16[1024,1024]{1,0:T(8,128)(2,1)} %bitcast.10, bf16[1024,1024]{1,0:T(8,128)(2,1)} %bitcast.11, bf16[8192,128]{1,0:T(8,128)(2,1)} %bitcast.12, s32[4,32,64]{2,1,0:T(8,128)} %bitcast.13), custom_call_target="tpu_custom_call" | custom-call | tf_op jit(solution)/shard_map/pallas_call | solution.py:647
  99.0 1.5 %shard_map.78 = (f32[16,1024]{1,0:T(8,128)}, f32[128,128]{1,0:T(8,128)}) custom-call(f32[16,1024]{1,0:T(8,128)} %get-tuple-element.6.a_ref, f32[128,128]{1,0:T(8,128)} %get-tuple-element.7.b_ref), custom_call_target="tpu_custom_call" | custom-call | tf_op jit(solution)/shard_map/pallas_call | solution.py:710

commit v5 on v4

--- a/solution.py
+++ b/solution.py
@@ -41,8 +41,8 @@
     pc = lax.axis_index("owner_2")
     rows = pre_v.shape[0] // (micros * sections)
     fine = rows // 2
-    small = 2 * sections
-    chunks = small + (micros - 1) * sections
+    group = 2 * sections
+    chunks = group * micros
     hidden = w_v.shape[0]
     lanes = emb_v.shape[1]
     last = section == sections - 1
@@ -50,29 +50,21 @@
     def part(ref, t, size):
         return ref.at[pl.ds(pl.multiple_of(t * size, size), size)]
 
-    def spot(t, size):
-        start = t * fine if size == fine else small * fine + (t - small) * rows
-        return pl.ds(pl.multiple_of(start, fine), size)
+    def spot(t):
+        return pl.ds(pl.multiple_of(t * fine, fine), fine)
 
     def each_chunk(body):
-        def narrow(t, carry):
-            body(t, fine)
-            return carry
-
-        def broad(t, carry):
-            body(t, rows)
-            return carry
-
-        lax.fori_loop(0, small, narrow, 0)
-        lax.fori_loop(small, chunks, broad, 0)
-
-    def pre_copy(t, size):
-        at = spot(t, size)
-        return pltpu.make_async_copy(pre_hbm.at[at], pre_v.at[at], pre_sem.at[t])
-
-    def cot_copy(t, size):
-        at = spot(t, size)
-        return pltpu.make_async_copy(cot_hbm.at[at], rbuf.at[at], in_sem.at[t])
+        def one(t, carry):
+            body(t)
+            return carry
+
+        lax.fori_loop(0, chunks, one, 0)
+
+    def pre_copy(t):
+        return pltpu.make_async_copy(pre_hbm.at[spot(t)], pre_v.at[spot(t)], pre_sem.at[t])
+
+    def cot_copy(t):
+        return pltpu.make_async_copy(cot_hbm.at[spot(t)], rbuf.at[spot(t)], in_sem.at[t])
 
     def remote(src, dst, send, recv, where):
         return pltpu.make_async_remote_copy(
@@ -80,24 +72,21 @@
             device_id=where, device_id_type=MESH,
         )
 
-    def down_copy(t, size):
-        at = spot(t, size)
+    def down_copy(t):
         return remote(
-            sbuf.at[at], rbuf.at[at], out_sem.at[t], in_sem.at[t],
+            sbuf.at[spot(t)], rbuf.at[spot(t)], out_sem.at[t], in_sem.at[t],
             {"section": lax.rem(section + sections - 1, sections)},
         )
 
-    def p_place(t, size):
-        if size == fine:
-            return t // 2, 0, lax.rem(t, 2) * fine
-        unit = (t - small) // sections + 1
-        return lax.rem(t, sections), unit, unit * rows
-
-    def p_copy(t, size):
-        to, unit, start = p_place(t, size)
+    def p_place(t):
+        unit = t // group
+        start = unit * rows + lax.rem(t, 2) * fine
+        return lax.rem(t, group) // 2, unit, pl.ds(pl.multiple_of(start, fine), fine)
+
+    def p_copy(t):
+        to, unit, at = p_place(t)
         return remote(
-            sbuf.at[spot(t, size)], pbuf.at[pl.ds(pl.multiple_of(start, fine), size)],
-            p_send.at[t], p_recv.at[unit], {"section": to},
+            sbuf.at[spot(t)], pbuf.at[at], p_send.at[t], p_recv.at[unit], {"section": to}
         )
 
     def chip(n):
@@ -110,20 +99,6 @@
     x_copy = pltpu.make_async_copy(x_hbm, x_v, x_sem)
     emb_copy = pltpu.make_async_copy(emb_hbm, emb_v, emb_sem)
     ids_copy = pltpu.make_async_copy(ids_hbm, raw_v, ids_sem)
-    w_copy.start()
-
-    def begin(t, size):
-        pre_copy(t, size).start()
-
-        @pl.when(last)
-        def _():
-            cot_copy(t, size).start()
-
-    each_chunk(begin)
-    ids_copy.start()
-    emb_copy.start()
-    x_copy.start()
-
     barrier = pltpu.get_barrier_semaphore()
 
     def peers(name, place, count, sem):
@@ -139,6 +114,23 @@
     def _():
         for name, place, count in inner:
             peers(name, place, count, barrier)
+
+    w_copy.start()
+
+    def begin(t):
+        pre_copy(t).start()
+
+        @pl.when(last)
+        def _():
+            cot_copy(t).start()
+
+    each_chunk(begin)
+    ids_copy.start()
+    emb_copy.start()
+    x_copy.start()
+
+    @pl.when(section == 0)
+    def _():
         pl.semaphore_wait(barrier, sections - 1 + sum(count - 1 for name, place, count in inner))
 
     @pl.when(section > 0)
@@ -230,18 +222,18 @@
         lax.fori_loop(0, hidden // 128, turn, 0)
         prepare()
 
-    def chain_step(t, size):
-        pre_copy(t, size).wait()
+    def chain_step(t):
+        pre_copy(t).wait()
 
         @pl.when(last)
         def _():
-            cot_copy(t, size).wait()
+            cot_copy(t).wait()
 
         @pl.when(jnp.logical_not(last))
         def _():
-            down_copy(t, size).wait_recv()
-
-        at = spot(t, size)
+            down_copy(t).wait_recv()
+
+        at = spot(t)
         incoming = rbuf[at, :]
         slope = jnp.where(pre_v[at, :] > 0, incoming, jnp.zeros_like(incoming))
         slopes[at, :] = slope
@@ -256,17 +248,17 @@
 
         @pl.when(section > 0)
         def _():
-            down_copy(t, size).start()
-
-        to, unit, start = p_place(t, size)
+            down_copy(t).start()
+
+        to, unit, place = p_place(t)
 
         @pl.when((section == 0) & (to > 0))
         def _():
-            p_copy(t, size).start()
+            p_copy(t).start()
 
         @pl.when((section == 0) & (to == 0))
         def _():
-            pbuf[pl.ds(pl.multiple_of(start, fine), size), :] = sbuf[at, :]
+            pbuf[place, :] = sbuf[at, :]
 
     block = 256
 
@@ -410,7 +402,7 @@
             fg[i, :, GROUP * g:GROUP * g + GROUP, :] = out.astype(BF16).reshape(features, GROUP, lanes)
 
         core = lax.rem(i, 2)
-        def send(step, carry):
+        def send(step):
             tx, cz, k, own_chip, feature = gather_at(nx * nz - 1 - step)
             arrived = f_recv.at[i // 2, px, jnp.where(k >= near_z, 1, 0)]
             src = fg.at[i, feature]
@@ -426,26 +418,33 @@
             def _():
                 remote(src, dst, f_send.at[i], arrived,
                        {"owner_0": tx, "owner_1": cz, "owner_2": core}).start()
-            return carry
-
-        lax.fori_loop(0, nx * nz, send, 0)
+
+        for step in range(nx * nz):
+            send(step)
 
     table_rows = acc.shape[1]
+
+    def mark_rows(i):
+        row = lax.broadcasted_iota(jnp.int32, (table_rows, 2 * rows), 0)
+
+        def mark(g, carry):
+            for z in range(nz):
+                both = idr[(g * nz + z) * 2] + idr[(g * nz + z) * 2 + 1]
+                ids = jnp.where(i < 2, both[:, :2 * rows], both[:, 2 * rows:])
+                onehot[g, :, z * 2 * rows:(z + 1) * 2 * rows] = jnp.where(row == ids, 1.0, 0.0).astype(BF16)
+            return carry
+
+        lax.fori_loop(0, nx, mark, 0)
 
     def table_part(i, role):
         h = i // 2
-        row = lax.broadcasted_iota(jnp.int32, (table_rows, 2 * rows), 0)
         low, high = ((0, near_z), (near_z, nz))[role]
         span = pl.ds(low * 2 * rows, (high - low) * 2 * rows)
 
         def gather(g, carry):
             landed = arr.at[h, g, span]
             pltpu.make_async_copy(landed, landed, f_recv.at[h, g, role]).wait()
-            for z in range(low, high):
-                both = idr[(g * nz + z) * 2] + idr[(g * nz + z) * 2 + 1]
-                ids = jnp.where(h == 0, both[:, :2 * rows], both[:, 2 * rows:])
-                onehot[:, z * 2 * rows:(z + 1) * 2 * rows] = jnp.where(row == ids, 1.0, 0.0).astype(BF16)
-            acc[role] = acc[role] + dot(onehot[:, span], arr[h, g, span, :], NN)
+            acc[role] = acc[role] + dot(onehot[g, :, span], arr[h, g, span, :], NN)
             return carry
 
         lax.fori_loop(0, nx, gather, 0)
@@ -457,17 +456,15 @@
         return chosen
 
     features_at = (
-        (by_section(8, 9, 12, 21), by_section(9, 10, 13, 21)),
-        (by_section(10, 13, 16, 26), by_section(12, 14, 17, 26)),
-        (by_section(13, 17, 21, 30), by_section(14, 18, 21, 30)),
-        (by_section(17, 21, 23, 34), by_section(18, 21, 23, 34)),
+        (by_section(8, 11, 17, 22), by_section(10, 13, 18, 22)),
+        (by_section(12, 20, 26, 38), by_section(14, 22, 27, 38)),
+        (by_section(18, 28, 33, 42), by_section(20, 30, 33, 42)),
+        (by_section(26, 33, 35, 46), by_section(28, 33, 35, 46)),
     )
-    far_table = jnp.where(pc == 0, by_section(15, 22, 22, 31), by_section(21, 22, 22, 35))
-    own_table = far_table + by_section(1, 0, 0, 0)
-    meet_time = by_section(5, 8, 10, 19)
-    x_time = by_section(20, 20, 20, 22)
-    z_time = by_section(40, 40, 40, 27)
-    ends = 36
+    table_at = jnp.where(pc == 0, by_section(34, 34, 34, 43), by_section(34, 34, 34, 47))
+    meet_time = by_section(5, 8, 12, 20)
+    x_time = by_section(33, 33, 36, 46)
+    ends = 48
 
     def tick(now, carry):
         for stage in range(3):
@@ -475,13 +472,9 @@
             def _():
                 meet(stage)
 
-        @pl.when(now < small)
-        def _():
-            chain_step(now, fine)
-
-        @pl.when((now >= small) & (now < chunks))
-        def _():
-            chain_step(now, rows)
+        @pl.when(now < chunks)
+        def _():
+            chain_step(now)
 
         @pl.when(now == meet_time)
         def _():
@@ -491,14 +484,14 @@
         def _():
             prepare()
 
-        done = now + 1 - small
-
-        @pl.when((now < chunks) & (done >= 0) & (lax.rem(done, sections) == 0))
-        def _():
-            @pl.when(done == 0)
+        done = now + 1
+
+        @pl.when((now < chunks) & (lax.rem(done, group) == 0))
+        def _():
+            @pl.when(done == group)
             def _():
                 x_copy.wait()
-            weight_step(done // sections)
+            weight_step(done // group - 1)
 
         @pl.when(now == chunks)
         def _():
@@ -518,22 +511,17 @@
         def _():
             feature_close(closed)
 
-        @pl.when(now == far_table)
+        @pl.when(now == table_at)
         def _():
             pltpu.make_async_copy(idr, idr, id_recv).wait()
+            mark_rows(pc)
             table_part(pc, 1)
-
-        @pl.when(now == own_table)
-        def _():
             table_part(pc, 0)
 
         @pl.when(now == x_time)
         def _():
             weight_x()
 
-        @pl.when(now == z_time)
-        def _():
-            weight_z()
         return carry
 
     lax.fori_loop(0, ends, tick, 0)
@@ -557,14 +545,13 @@
         for d in range(1, sections):
             y_copy(d, q).start()
 
+    mark_rows(2 + pc)
     table_part(2 + pc, 1)
     sib_copy(1).start()
     table_part(2 + pc, 0)
     sib_copy(0).start()
 
-    @pl.when(z_time > ends)
-    def _():
-        weight_z()
+    weight_z()
 
     settle(1)
     settle(0)
@@ -584,14 +571,14 @@
     far_copy.wait_recv()
     tg_out[...] = (total + frecv[...].astype(F32)) * scale
 
-    def finish(t, size):
+    def finish(t):
         @pl.when(section > 0)
         def _():
-            down_copy(t, size).wait_send()
-
-        @pl.when((section == 0) & (p_place(t, size)[0] > 0))
-        def _():
-            p_copy(t, size).wait_send()
+            down_copy(t).wait_send()
+
+        @pl.when((section == 0) & (p_place(t)[0] > 0))
+        def _():
+            p_copy(t).wait_send()
 
     each_chunk(finish)
     some = pl.ds(0, 2 * nx * nz - 2)
@@ -637,7 +624,7 @@
     dma = pltpu.SemaphoreType.DMA
     vmem = pl.BlockSpec(memory_space=pltpu.VMEM)
     hbm = pl.BlockSpec(memory_space=pl.ANY)
-    chunks = (micros + 1) * sections
+    chunks = 2 * sections * micros
     rows = total // (micros * sections)
     wide = GROUP * features
     part = hidden // owners
@@ -646,10 +633,7 @@
     V = pltpu.VMEM
     weight_grad, table_grad = pl.pallas_call(
         functools.partial(step_kernel, (micros, sections, nx, nz, features), scale),
-        out_shape=(
-            jax.ShapeDtypeStruct((part, hidden), F32),
-            jax.ShapeDtypeStruct((half // sections, width), F32),
-        ),
+        out_shape=(V((part, hidden), F32), V((half // sections, width), F32)),
         in_specs=[hbm] * 6,
         out_specs=(vmem, vmem),
         scratch_shapes=[
@@ -681,7 +665,7 @@
             V((micros, features, rows, width), BF16),
             V((micros // 2, nx, nz * 2 * rows, width), BF16),
             V(ids_shape, jnp.int32),
-            V((table_rows, nz * 2 * rows), BF16),
+            V((nx, table_rows, nz * 2 * rows), BF16),
             V((2, table_rows, width), F32),
             V((2, half, width), F32),
             V((2, half, width), BF16),
@@ -715,7 +699,7 @@
         ),
         in_specs=[vmem] * 2,
         out_specs=(vmem, vmem),
-    )(weight_grad, table_grad)
+    )(pltpu.with_memory_space_constraint(weight_grad, pltpu.VMEM), pltpu.with_memory_space_constraint(table_grad, pltpu.VMEM))
     return (weight_grad[None], table_grad[None])
 
 

time: 101 us -> 97.9 us (0.969)
  Pallas kernels: 99.9 us -> 95.9 us
    pallas_call x1, Pallas kernels: 98.4 us -> 95.2 us  [per_device(): pl.pallas_call(functools.partial(step_kernel, (micros, sections, nx, nz,...]
where the time goes in v5:
time: 97.9 us; the launch traced here: 96.5 us
  Pallas kernels  95.9 us (98%)
    pallas_call x1, Pallas kernels, per_device(): pl.pallas_call(functools.partial(step_kernel, (micros, sections, nx, nz,...  95.2 us

profile of v5, /device:TPU:1, one launch (start us, length us, event | category | flops | bytes accessed | tf_op | source)
XLA Modules:
  0.0 96.5 jit_solution(313937570142308662)
XLA Ops:
  0.6 95.2 %shard_map.77 = (f32[16,1024]{1,0:T(8,128)S(1)}, f32[128,128]{1,0:T(8,128)S(1)}) custom-call(bf16[1024,1024]{1,0:T(8,128)(2,1)} %bitcast.8, bf16[1024,1024]{1,0:T(8,128)(2,1)} %bitcast.9, bf16[1024,1024]{1,0:T(8,128)(2,1)} %bitcast.10, bf16[1024,1024]{1,0:T(8,128)(2,1)} %bitcast.11, bf16[8192,128]{1,0:T(8,128)(2,1)} %bitcast.12, s32[4,32,64]{2,1,0:T(8,128)} %bitcast.13), custom_call_target="tpu_custom_call" | custom-call | tf_op jit(solution)/shard_map/pallas_call | solution.py:634
  95.9 0.7 shard_map.78

commit v6 on v5

--- a/solution.py
+++ b/solution.py
@@ -461,7 +461,8 @@
         (by_section(18, 28, 33, 42), by_section(20, 30, 33, 42)),
         (by_section(26, 33, 35, 46), by_section(28, 33, 35, 46)),
     )
-    table_at = jnp.where(pc == 0, by_section(34, 34, 34, 43), by_section(34, 34, 34, 47))
+    mark_at = by_section(22, 34, 34, 43)
+    table_at = by_section(34, 34, 34, 43)
     meet_time = by_section(5, 8, 12, 20)
     x_time = by_section(33, 33, 36, 46)
     ends = 48
@@ -511,10 +512,13 @@
         def _():
             feature_close(closed)
 
-        @pl.when(now == table_at)
+        @pl.when(now == mark_at)
         def _():
             pltpu.make_async_copy(idr, idr, id_recv).wait()
             mark_rows(pc)
+
+        @pl.when(now == table_at)
+        def _():
             table_part(pc, 1)
             table_part(pc, 0)
 
@@ -550,10 +554,8 @@
     sib_copy(1).start()
     table_part(2 + pc, 0)
     sib_copy(0).start()
-
+    settle(1)
     weight_z()
-
-    settle(1)
     settle(0)
 
     def gathered(q):

time: 97.9 us -> 96.2 us (0.983)
  Pallas kernels: 95.9 us -> 93.8 us
    pallas_call x1, Pallas kernels: 95.2 us -> 93.1 us  [per_device(): pl.pallas_call(functools.partial(step_kernel, (micros, sections, nx, nz,...]
where the time goes in v6:
time: 96.2 us; the launch traced here: 94.4 us
  Pallas kernels  93.8 us (98%)
    pallas_call x1, Pallas kernels, per_device(): pl.pallas_call(functools.partial(step_kernel, (micros, sections, nx, nz,...  93.1 us

profile of v6, /device:TPU:1, one launch (start us, length us, event | category | flops | bytes accessed | tf_op | source)
XLA Modules:
  0.0 94.4 jit_solution(1412564781472991490)
XLA Ops:
  0.6 93.1 %shard_map.77 = (f32[16,1024]{1,0:T(8,128)S(1)}, f32[128,128]{1,0:T(8,128)S(1)}) custom-call(bf16[1024,1024]{1,0:T(8,128)(2,1)} %bitcast.8, bf16[1024,1024]{1,0:T(8,128)(2,1)} %bitcast.9, bf16[1024,1024]{1,0:T(8,128)(2,1)} %bitcast.10, bf16[1024,1024]{1,0:T(8,128)(2,1)} %bitcast.11, bf16[8192,128]{1,0:T(8,128)(2,1)} %bitcast.12, s32[4,32,64]{2,1,0:T(8,128)} %bitcast.13), custom_call_target="tpu_custom_call" | custom-call | tf_op jit(solution)/shard_map/pallas_call | solution.py:636
  93.8 0.7 shard_map.78

commit v7 on v6

--- a/solution.py
+++ b/solution.py
@@ -631,7 +631,7 @@
     wide = GROUP * features
     part = hidden // owners
     half = table_rows // 2
-    cut = hidden * 3 // 4
+    cut = hidden * 5 // 8
     V = pltpu.VMEM
     weight_grad, table_grad = pl.pallas_call(
         functools.partial(step_kernel, (micros, sections, nx, nz, features), scale),

time: 96.2 us -> 94.3 us (0.980); the launches traced: 94.4 us -> 94.1 us
  no operation moved by 1% of the time
where the time goes in v7:
time: 94.3 us; the launch traced here: 94.1 us
  Pallas kernels  93.5 us (99%)
    pallas_call x1, Pallas kernels, per_device(): pl.pallas_call(functools.partial(step_kernel, (micros, sections, nx, nz,...  92.8 us

profile of v7, /device:TPU:1, one launch (start us, length us, event | category | flops | bytes accessed | tf_op | source)
XLA Modules:
  0.0 94.1 jit_solution(9868366220586177316)
XLA Ops:
  0.6 92.8 %shard_map.77 = (f32[16,1024]{1,0:T(8,128)S(1)}, f32[128,128]{1,0:T(8,128)S(1)}) custom-call(bf16[1024,1024]{1,0:T(8,128)(2,1)} %bitcast.8, bf16[1024,1024]{1,0:T(8,128)(2,1)} %bitcast.9, bf16[1024,1024]{1,0:T(8,128)(2,1)} %bitcast.10, bf16[1024,1024]{1,0:T(8,128)(2,1)} %bitcast.11, bf16[8192,128]{1,0:T(8,128)(2,1)} %bitcast.12, s32[4,32,64]{2,1,0:T(8,128)} %bitcast.13), custom_call_target="tpu_custom_call" | custom-call | tf_op jit(solution)/shard_map/pallas_call | solution.py:636
  93.4 0.7 shard_map.78
